TPU v7x, 16 devices: a whole 2x2x2 slice. The times are simulated.
16 devices in a mesh: dp: 4 (over z, y), sp: 4 (over x, core).
Axes of the slice: x: 2, y: 2, z: 2, core: 2. Of those that a mesh axis runs over, the one named last changes fastest.
Arguments:
- x_rows: bfloat16 [32768, 384], P(('dp', 'sp')), parts along dimension 0
- dy_rows: bfloat16 [32768, 384], P(('dp', 'sp')), parts along dimension 0
- ln_gamma: float32 [384], replicated
- ln_beta: float32 [384], replicated
- w_qkv: bfloat16 [384, 1152], replicated
- w_out: bfloat16 [384, 384], replicated
- temperature: float32 [8], replicated
Outputs:
- output 1: bfloat16 [32768, 384], P(('dp', 'sp')), parts along dimension 0
- output 2: bfloat16 [32768, 384], P(('dp', 'sp')), parts along dimension 0
- output 3: bfloat16 [1536, 1152], P(('dp', 'sp')), parts along dimension 0
- output 4: bfloat16 [1536, 384], P(('dp', 'sp')), parts along dimension 0
- output 5: float32 [1536], P('dp'), parts along dimension 0
- output 6: float32 [1536], P('dp'), parts along dimension 0
- output 7: float32 [32], P('dp'), parts along dimension 0
There are 4 independent parts. A program takes and returns all parts, laid end to end along the dimension named above; an argument that names none is the same for every part.
All inputs are finite; a program needn't handle non-finite values.
Results may differ from a plain program's by a relative error of at most 0.0117443.
Values are sent between devices in bfloat16 or wider.
A program may use at most 1 GiB of HBM per device.

v0:
```python
import jax
import jax.numpy as jnp
from jax import lax
from jax.sharding import PartitionSpec as P

LN_EPS = 1e-6


def layer_norm_fwd(x_rows, ln_gamma, ln_beta):
    x_f32 = x_rows.astype(jnp.float32)
    centered = x_f32 - jnp.mean(x_f32, axis=-1, keepdims=True)
    inv_std = lax.rsqrt(jnp.mean(centered * centered, axis=-1, keepdims=True) + LN_EPS)
    x_hat = centered * inv_std
    normed = (x_hat * ln_gamma + ln_beta).astype(jnp.bfloat16)
    return normed, x_hat, inv_std


def layer_norm_bwd(d_normed, x_hat, inv_std, ln_gamma):
    d_f32 = d_normed.astype(jnp.float32)
    d_gamma_part = jnp.sum(d_f32 * x_hat, axis=0)
    d_beta_part = jnp.sum(d_f32, axis=0)
    d_hat = d_f32 * ln_gamma
    d_x = inv_std * (d_hat - jnp.mean(d_hat, axis=-1, keepdims=True) - x_hat * jnp.mean(d_hat * x_hat, axis=-1, keepdims=True))
    return d_x, d_gamma_part, d_beta_part


def state_softmax(gram, q_sq, k_sq, value_a11):
    q_inv = lax.rsqrt(q_sq)[:, :, None]
    k_inv = lax.rsqrt(k_sq)[:, None, :]
    scores = value_a11[:, None, None] * gram * q_inv * k_inv
    return jax.nn.softmax(scores, axis=-1), scores


def state_softmax_bwd(d_attn, attn_f32, scores, gram, q_sq, k_sq, value_a11):
    d_scores = attn_f32 * (d_attn - jnp.sum(d_attn * attn_f32, axis=-1, keepdims=True))
    q_inv = lax.rsqrt(q_sq)[:, :, None]
    k_inv = lax.rsqrt(k_sq)[:, None, :]
    d_temp = jnp.sum(d_scores * gram * q_inv * k_inv, axis=(1, 2))
    d_gram = (d_scores * value_a11[:, None, None] * q_inv * k_inv).astype(jnp.bfloat16)
    weighted = d_scores * scores
    d_q_sq = -0.5 * jnp.sum(weighted, axis=2) / q_sq
    d_k_sq = -0.5 * jnp.sum(weighted, axis=1) / k_sq
    return d_gram, d_q_sq, d_k_sq, d_temp


def xca_local(x_rows, dy_rows, ln_gamma, ln_beta, w_qkv, w_out, value_a11):
    n_local, model_width = x_rows.shape
    n_heads = value_a11.shape[0]
    head_dim = model_width // n_heads
    normed, x_hat, inv_std = layer_norm_fwd(x_rows, ln_gamma, ln_beta)
    qkv_all = jnp.dot(normed, w_qkv, preferred_element_type=jnp.float32).astype(jnp.bfloat16)
    qkv_heads = qkv_all.reshape(n_local, 3, n_heads, head_dim)
    query_h = qkv_heads[:, 0]
    key_h = qkv_heads[:, 1]
    value_h = qkv_heads[:, 2]
    gram_part = jnp.einsum('nhi,nhj->hij', query_h, key_h, preferred_element_type=jnp.float32)
    q_sq_part = jnp.sum(jnp.square(query_h.astype(jnp.float32)), axis=0)
    k_sq_part = jnp.sum(jnp.square(key_h.astype(jnp.float32)), axis=0)
    gram, q_sq, k_sq = lax.psum((gram_part, q_sq_part, k_sq_part), 'sp')
    attn_f32, scores = state_softmax(gram, q_sq, k_sq, value_a11)
    attn = attn_f32.astype(jnp.bfloat16)
    attn_out = jnp.einsum('nhj,hij->nhi', value_h, attn, preferred_element_type=jnp.float32).astype(jnp.bfloat16)
    out_flat = attn_out.reshape(n_local, model_width)
    y_rows = (x_rows.astype(jnp.float32) + jnp.dot(out_flat, w_out, preferred_element_type=jnp.float32)).astype(jnp.bfloat16)

    d_out = jnp.einsum('nc,dc->nd', dy_rows, w_out, preferred_element_type=jnp.float32).astype(jnp.bfloat16)
    dw_out_part = jnp.einsum('nd,nc->dc', out_flat, dy_rows, preferred_element_type=jnp.float32)
    d_out_h = d_out.reshape(n_local, n_heads, head_dim)
    d_attn_part = jnp.einsum('nhi,nhj->hij', d_out_h, value_h, preferred_element_type=jnp.float32)
    d_attn = lax.psum(d_attn_part, 'sp').astype(jnp.bfloat16).astype(jnp.float32)
    d_gram, d_q_sq, d_k_sq, d_temp = state_softmax_bwd(d_attn, attn_f32, scores, gram, q_sq, k_sq, value_a11)
    d_query = jnp.einsum('hij,nhj->nhi', d_gram, key_h, preferred_element_type=jnp.float32) + 2.0 * query_h.astype(jnp.float32) * d_q_sq
    d_key = jnp.einsum('hij,nhi->nhj', d_gram, query_h, preferred_element_type=jnp.float32) + 2.0 * key_h.astype(jnp.float32) * d_k_sq
    d_value = jnp.einsum('nhi,hij->nhj', d_out_h, attn, preferred_element_type=jnp.float32)
    d_qkv = jnp.stack([d_query, d_key, d_value], axis=1).astype(jnp.bfloat16).reshape(n_local, 3 * model_width)
    d_normed = jnp.einsum('nc,dc->nd', d_qkv, w_qkv, preferred_element_type=jnp.float32).astype(jnp.bfloat16)
    dw_qkv_part = jnp.einsum('nd,nc->dc', normed, d_qkv, preferred_element_type=jnp.float32)
    d_ln, d_gamma_part, d_beta_part = layer_norm_bwd(d_normed, x_hat, inv_std, ln_gamma)
    dx_rows = (dy_rows.astype(jnp.float32) + d_ln).astype(jnp.bfloat16)
    dw_qkv = lax.psum_scatter(dw_qkv_part, 'sp', scatter_dimension=0, tiled=True).astype(jnp.bfloat16)
    dw_out = lax.psum_scatter(dw_out_part, 'sp', scatter_dimension=0, tiled=True).astype(jnp.bfloat16)
    d_gamma, d_beta = lax.psum((d_gamma_part, d_beta_part), 'sp')
    return y_rows, dx_rows, dw_qkv, dw_out, d_gamma, d_beta, d_temp


def solution(mesh):
    row_spec = P(('dp', 'sp'), None)
    full_mat = P(None, None)
    full_vec = P(None)
    part_vec = P('dp')
    return jax.shard_map(xca_local, mesh=mesh, in_specs=(row_spec, row_spec, full_vec, full_vec, full_mat, full_mat, full_vec), out_specs=(row_spec, row_spec, row_spec, row_spec, part_vec, part_vec, part_vec), check_vma=False)
```

profile of v0, /device:TPU:0, one launch (start us, length us, event | category | flops | bytes accessed | tf_op | source)
XLA Modules:
  0.0 120.1 jit_solution(8961617497856927656)
XLA Ops:
  7.3 1.9 %convert_reduce_fusion.1 = f32[2048]{0:T(1024)S(1)} fusion(bf16[2048,384]{1,0:T(8,128)(2,1)} %param.7), kind=kLoop, calls=%fused_computation.8 | loop fusion | flops 1570816 | bytes 1581056 | tf_op jit(solution)/shard_map/reduce_sum | solution.py:11
  9.2 2.2 %fusion.15 = f32[2048]{0:T(1024)S(1)} fusion(bf16[2048,384]{1,0:T(8,128)(2,1)} %param.7, f32[2048]{0:T(1024)S(1)} %broadcast_multiply_fusion.2), kind=kLoop, calls=%fused_computation.27 | loop fusion | flops 3143680 | bytes 1589248 | tf_op jit(solution)/shard_map/reduce_sum | solution.py:12
  11.4 3.3 %convolution_convert_fusion = bf16[2048,1152]{0,1:T(8,128)(2,1)S(1)} fusion(bf16[384,1152]{1,0:T(8,128)(2,1)S(1)} %copy-done, bf16[2048,384]{1,0:T(8,128)(2,1)S(1)} %copy-done.1, f32[384]{0:T(512)S(1)} %copy-done.12, f32[384]{0:T(512)S(1)} %copy-done.11, f32[2048]{0:T(1024)S(1)} %add_rsqrt_fusion, f32[2048]{0:T(1024)S(1)} %broadcast_multiply_fusion.2), kind=kOutput, calls=%fused_computation.2 | convolution fusion | flops 1819017216 | bytes 7195648 | tf_op jit(solution)/shard_map/dot_general | solution.py:51
  14.8 2.1 %copy-done.4 = bf16[2048,1152]{0,1:T(8,128)(2,1)} copy-done((bf16[2048,1152]{0,1:T(8,128)(2,1)}, bf16[2048,1152]{0,1:T(8,128)(2,1)S(1)}, u32[]{:S(2)}) %copy-start.4) | copy-done | bytes 4718616
  18.2 2.6 %convolution_convert_fusion.3 = bf16[2048,384]{0,1:T(8,128)(2,1)S(1)} fusion(bf16[2048,384]{1,0:T(8,128)(2,1)} %param.8, bf16[384,384]{1,0:T(8,128)(2,1)S(1)} %copy-done.9), kind=kOutput, calls=%fused_computation.39 | convolution fusion | flops 604766208 | bytes 3440640 | tf_op jit(solution)/shard_map/nc,dc->nd/dot_general | solution.py:66
  23.4 16.3 %all-reduce.1 = (f32[8,48]{1,0:T(8,128)S(1)}, f32[8,48]{1,0:T(8,128)S(1)}, bf16[8,48,48]{2,1,0:T(8,128)(2,1)S(1)}) all-reduce(f32[8,48]{1,0:T(8,128)S(1)} %get-tuple-element.8, f32[8,48]{1,0:T(8,128)S(1)} %get-tuple-element.7, f32[8,48,48]{2,1,0:T(8,128)S(1)} %fusion.28), channel_id=1, replica_groups=mesh['dp'=4,'sp'=4] {'sp'}, use_global_device_ids=true, to_apply=%region_6.0 | all-reduce | flops 19200 | bytes 116736 | tf_op jit(solution)/shard_map/psum | solution.py:59
  39.7 9.8 %all-reduce.4.cloned.1.call-done = f32[8,48,48]{2,1,0:T(8,128)} async-done(((f32[8,48,48]{2,1,0:T(8,128)}), f32[8,48,48]{2,1,0:T(8,128)}) %all-reduce.4.cloned.1.call-update) | async-done | bytes 73744 | tf_op jit(solution)/shard_map/psum | solution.py:59
  49.5 2.3 %fusion.48 = (f32[8,48]{1,0:T(8,128)S(1)}, f32[8,48,48]{2,1,0:T(8,128)S(1)}) fusion(f32[8,48,48]{2,1,0:T(8,128)} %all-reduce.4.cloned.1.call-done, f32[8,48]{1,0:T(8,128)S(1)} %rsqrt.18, f32[8,48]{1,0:T(8,128)S(1)} %rsqrt.17, f32[8]{0:T(128)S(1)} %copy-done.10), kind=kOutput, calls=%fused_computation.76 | output fusion | flops 92207 | bytes 152096 | tf_op jit(solution)/shard_map/sub | solution.py:31
  51.8 4.2 %convolution_convert_fusion.4 = bf16[8,48,2048]{2,1,0:T(8,128)(2,1)} fusion(bf16[2048,3,8,48]{0,3,2,1:T(8,128)(2,1)} %bitcast.57, f32[8,48]{1,0:T(8,128)S(1)} %get-tuple-element.21, f32[8,48,48]{2,1,0:T(8,128)} %all-reduce.4.cloned.1.call-done, f32[8,48]{1,0:T(8,128)S(1)} %rsqrt.18, f32[8,48]{1,0:T(8,128)S(1)} %rsqrt.17, f32[8]{0:T(128)S(1)} %copy-done.10), kind=kOutput, calls=%fused_computation.40 | convolution fusion | flops 76394928 | bytes 3346976 | tf_op jit(solution)/shard_map/nhj,hij->nhi/dot_general | solution.py:62
  56.0 3.8 %fusion.49 = f32[384,384]{1,0:T(8,128)} fusion(bf16[2048,384]{0,1:T(8,128)(2,1)} %bitcast.64, bf16[2048,384]{1,0:T(8,128)(2,1)} %param.8), kind=kOutput, calls=%fused_computation.77 | convolution fusion | flops 603979776 | bytes 3735552 | tf_op jit(solution)/shard_map/nd,nc->dc/dot_general | solution.py:67
  60.0 2.6 %fusion.44 = (f32[8,48]{1,0:T(8,128)S(1)}, f32[8,48]{1,0:T(8,128)S(1)}, f32[8]{0:T(128)}) fusion(f32[8,48]{1,0:T(8,128)S(1)} %rsqrt.18, f32[8,48]{1,0:T(8,128)S(1)} %rsqrt.17, f32[8,48,48]{2,1,0:T(8,128)S(1)} %copy-done.8, f32[8]{0:T(128)S(1)} %copy-done.10, bf16[8,48,48]{2,1,0:T(8,128)(2,1)S(1)} %get-tuple-element.20, ...), kind=kOutput, calls=%fused_computation.74 | output fusion | flops 312999 | bytes 192064 | tf_op jit(solution)/shard_map/sub | solution.py:35
  62.7 5.4 %fusion.26 = bf16[2048,1,8,48]{0,3,2,1:T(8,128)(2,1)} fusion(f32[8,48]{1,0:T(8,128)S(1)} %get-tuple-element.24, bf16[2048,3,8,48]{0,3,2,1:T(8,128)(2,1)} %bitcast.58, f32[8,48]{1,0:T(8,128)S(1)} %rsqrt.18, f32[8,48]{1,0:T(8,128)S(1)} %rsqrt.17, f32[8]{0:T(128)S(1)} %copy-done.10, bf16[8,48,48]{2,1,0:T(8,128)(2,1)S(1)} %get-tuple-element.20, ...), kind=kOutput, calls=%fused_computation.42 | convolution fusion | flops 78846384 | bytes 5329408 | tf_op jit(solution)/shard_map/hij,nhi->nhj/dot_general | solution.py:73
  68.1 5.1 %fusion.27 = bf16[2048,1,8,48]{0,3,2,1:T(8,128)(2,1)} fusion(f32[8,48]{1,0:T(8,128)S(1)} %get-tuple-element.25, bf16[2048,3,8,48]{0,3,2,1:T(8,128)(2,1)} %bitcast.59, f32[8,48]{1,0:T(8,128)S(1)} %rsqrt.18, f32[8,48]{1,0:T(8,128)S(1)} %rsqrt.17, f32[8]{0:T(128)S(1)} %copy-done.10, bf16[8,48,48]{2,1,0:T(8,128)(2,1)S(1)} %get-tuple-element.20, ...), kind=kOutput, calls=%fused_computation.43 | convolution fusion | flops 78846384 | bytes 5329408 | tf_op jit(solution)/shard_map/hij,nhj->nhi/dot_general | solution.py:72
  73.2 4.3 %fusion.25 = bf16[2048,1,8,48]{0,3,2,1:T(8,128)(2,1)} fusion(bf16[2048,8,48]{0,2,1:T(8,128)(2,1)} %bitcast.55, f32[8,48]{1,0:T(8,128)S(1)} %get-tuple-element.21, f32[8,48,48]{2,1,0:T(8,128)S(1)} %copy-done.8, f32[8,48]{1,0:T(8,128)S(1)} %rsqrt.18, f32[8,48]{1,0:T(8,128)S(1)} %rsqrt.17, f32[8]{0:T(128)S(1)} %copy-done.10), kind=kOutput, calls=%fused_computation.41 | convolution fusion | flops 76394928 | bytes 3224096 | tf_op jit(solution)/shard_map/nhi,hij->nhj/dot_general | solution.py:74
  77.5 2.6 %pad_maximum_fusion = bf16[2048,3,8,48]{0,3,2,1:T(8,128)(2,1)S(1)} fusion(bf16[2048,1,8,48]{0,3,2,1:T(8,128)(2,1)} %fusion.25, bf16[2048,1,8,48]{0,3,2,1:T(8,128)(2,1)} %fusion.26, bf16[2048,1,8,48]{0,3,2,1:T(8,128)(2,1)} %fusion.27), kind=kLoop, calls=%fused_computation.9 | loop fusion | flops 4718592 | bytes 9437184 | tf_op jit(solution)/shard_map/stack | solution.py:75
  80.1 2.1 %copy-done.6 = bf16[2048,3,8,48]{0,3,2,1:T(8,128)(2,1)} copy-done((bf16[2048,3,8,48]{0,3,2,1:T(8,128)(2,1)}, bf16[2048,3,8,48]{0,3,2,1:T(8,128)(2,1)S(1)}, u32[]{:S(2)}) %copy-start.6) | copy-done | bytes 4718616
  82.2 4.2 %fusion.45 = f32[384,1152]{1,0:T(8,128)} fusion(bf16[2048,1152]{0,1:T(8,128)(2,1)S(1)} %bitcast.62, bf16[2048,384]{1,0:T(8,128)(2,1)S(1)} %copy-done.1, f32[384]{0:T(512)S(1)} %copy-done.12, f32[384]{0:T(512)S(1)} %copy-done.11, f32[2048]{0:T(1024)S(1)} %add_rsqrt_fusion, f32[2048]{0:T(1024)S(1)} %broadcast_multiply_fusion.2), kind=kOutput, calls=%fused_computation.75 | convolution fusion | flops 1816657920 | bytes 8080384 | tf_op jit(solution)/shard_map/nd,nc->dc/dot_general | solution.py:77
  86.4 7.9 %fusion.24 = (f32[384]{0:T(512)S(1)}, f32[2048]{0:T(1024)S(1)}, f32[2048]{0:T(1024)S(1)}, f32[384]{0:T(512)S(1)}, bf16[2048,384]{1,0:T(8,128)(2,1)}) fusion(bf16[2048,384]{1,0:T(8,128)(2,1)S(1)} %copy-done.1, f32[2048]{0:T(1024)S(1)} %add_rsqrt_fusion, f32[2048]{0:T(1024)S(1)} %broadcast_multiply_fusion.2, f32[384]{0:T(512)S(1)} %copy-done.11, ...), kind=kOutput, calls=%fused_computation.36 | convolution fusion | flops 1821371648 | bytes 8786432 | tf_op jit(solution)/shard_map/nc,dc->nd/dot_general | solution.py:76
  94.3 6.3 %all-reduce = (f32[384]{0:T(512)}, f32[384]{0:T(512)}) all-reduce(f32[384]{0:T(512)S(1)} %get-tuple-element.9, f32[384]{0:T(512)S(1)} %get-tuple-element.12), channel_id=1, replica_groups=mesh['dp'=4,'sp'=4] {'sp'}, use_global_device_ids=true, to_apply=%region_18.0 | all-reduce | flops 768 | bytes 6144 | tf_op jit(solution)/shard_map/psum | solution.py:82
  100.7 3.9 %fusion.23 = bf16[2048,384]{1,0:T(8,128)(2,1)} fusion(bf16[2048,384]{1,0:T(8,128)(2,1)S(1)} %copy-done.1, bf16[2048,384]{0,1:T(8,128)(2,1)} %bitcast.65, bf16[384,384]{1,0:T(8,128)(2,1)S(1)} %copy-done.9), kind=kOutput, calls=%fused_computation.35 | convolution fusion | flops 606339072 | bytes 5013504 | tf_op jit(solution)/shard_map/dot_general | solution.py:64
  104.5 2.6 %fusion.14 = bf16[2048,384]{1,0:T(8,128)(2,1)} fusion(bf16[2048,384]{1,0:T(8,128)(2,1)S(1)} %copy-done.1, bf16[2048,384]{1,0:T(8,128)(2,1)S(1)} %copy-done.7, bf16[2048,384]{1,0:T(8,128)(2,1)S(1)} %copy-done.2, f32[2048]{0:T(1024)S(1)} %broadcast_multiply_fusion, f32[2048]{0:T(1024)S(1)} %broadcast_multiply_fusion.1, f32[384]{0:T(512)S(1)} %copy-done.11, ...), kind=kLoop, calls=%fused_computation.26 | loop fusion | flops 9437184 | bytes 6325760 | tf_op jit(solution)/shard_map/convert_element_type | solution.py:79
  107.2 1.6 %convert_element_type.84 = bf16[96,384]{1,0:T(8,128)(2,1)} convert(f32[96,384]{1,0:T(8,128)} %reduce-scatter.5.cloned.1.call-done) | non-fusion elementwise | flops 36864 | bytes 221184 | tf_op jit(solution)/shard_map/convert_element_type | solution.py:81
  108.7 3.1 %reduce-scatter.3.cloned.1.call-done = f32[96,1152]{1,0:T(8,128)} async-done(((f32[384,1152]{1,0:T(8,128)}), f32[96,1152]{1,0:T(8,128)}) %reduce-scatter.3.cloned.1.call-update) | async-done | bytes 442384 | tf_op jit(solution)/shard_map/reduce_scatter | solution.py:80
  111.9 1.7 %convert_element_type.83 = bf16[96,1152]{1,0:T(8,128)(2,1)} convert(f32[96,1152]{1,0:T(8,128)} %reduce-scatter.3.cloned.1.call-done) | non-fusion elementwise | flops 110592 | bytes 663552 | tf_op jit(solution)/shard_map/convert_element_type | solution.py:80
  (41 shorter events, 4.2 us)
Async XLA Ops:
  7.2 4.2 %copy-start = (bf16[384,1152]{1,0:T(8,128)(2,1)S(1)}, bf16[384,1152]{1,0:T(8,128)(2,1)}, u32[]{:S(2)}) copy-start(bf16[384,1152]{1,0:T(8,128)(2,1)} %param.11) | copy-start | bytes 2654212
  7.2 4.2 %copy-start.1 = (bf16[2048,384]{1,0:T(8,128)(2,1)S(1)}, bf16[2048,384]{1,0:T(8,128)(2,1)}, u32[]{:S(2)}) copy-start(bf16[2048,384]{1,0:T(8,128)(2,1)} %param.7) | copy-start | bytes 4718596
  7.2 4.2 %copy-start.11 = (f32[384]{0:T(512)S(1)}, f32[384]{0:T(512)}, u32[]{:S(2)}) copy-start(f32[384]{0:T(512)} %param.9) | copy-start | bytes 4612
  7.2 4.2 %copy-start.12 = (f32[384]{0:T(512)S(1)}, f32[384]{0:T(512)}, u32[]{:S(2)}) copy-start(f32[384]{0:T(512)} %param.10) | copy-start | bytes 4612
  7.2 42.3 %all-reduce.4.cloned.1.call-start = ((), (), s32[]{:S(2)}) async-start(), calls=%async_computation.2 | async-start | bytes 393216 | tf_op jit(solution)/shard_map/psum | solution.py:59
  14.8 2.1 %copy-start.4 = (bf16[2048,1152]{0,1:T(8,128)(2,1)}, bf16[2048,1152]{0,1:T(8,128)(2,1)S(1)}, u32[]{:S(2)}) copy-start(bf16[2048,1152]{0,1:T(8,128)(2,1)S(1)} %convolution_convert_fusion) | copy-start | bytes 14155780
  14.8 3.4 %copy-start.9 = (bf16[384,384]{1,0:T(8,128)(2,1)S(1)}, bf16[384,384]{1,0:T(8,128)(2,1)}, u32[]{:S(2)}) copy-start(bf16[384,384]{1,0:T(8,128)(2,1)} %param.12) | copy-start | bytes 884740
  18.2 89.0 %reduce-scatter.5.cloned.1.call-start = ((), (), s32[]{:S(2)}) async-start(), calls=%async_computation.4 | async-start | bytes 737280 | tf_op jit(solution)/shard_map/reduce_scatter | solution.py:81
  18.2 3.7 %copy-start.5 = (bf16[2048,1152]{0,1:T(8,128)(2,1)S(1)}, bf16[2048,1152]{0,1:T(8,128)(2,1)}, u32[]{:S(2)}) copy-start(bf16[2048,1152]{0,1:T(8,128)(2,1)} %copy-done.4) | copy-start | bytes 14155780
  20.8 1.1 copy-start.3
  22.0 27.5 %copy-start.10 = (f32[8]{0:T(128)S(1)}, f32[8]{0:T(128)}, u32[]{:S(2)}) copy-start(f32[8]{0:T(128)} %param.13) | copy-start | bytes 100
  56.0 4.0 %copy-start.8 = (f32[8,48,48]{2,1,0:T(8,128)S(1)}, f32[8,48,48]{2,1,0:T(8,128)}, u32[]{:S(2)}) copy-start(f32[8,48,48]{2,1,0:T(8,128)} %all-reduce.4.cloned.1.call-done) | copy-start | bytes 221188
  59.8 52.1 %reduce-scatter.3.cloned.1.call-start = ((), (), s32[]{:S(2)}) async-start(), calls=%async_computation.3 | async-start | bytes 2211840 | tf_op jit(solution)/shard_map/reduce_scatter | solution.py:80
  80.1 2.1 %copy-start.6 = (bf16[2048,3,8,48]{0,3,2,1:T(8,128)(2,1)}, bf16[2048,3,8,48]{0,3,2,1:T(8,128)(2,1)S(1)}, u32[]{:S(2)}) copy-start(bf16[2048,3,8,48]{0,3,2,1:T(8,128)(2,1)S(1)} %pad_maximum_fusion) | copy-start | bytes 14155780
  100.6 3.9 %copy-start.2 = (bf16[2048,384]{1,0:T(8,128)(2,1)S(1)}, bf16[2048,384]{1,0:T(8,128)(2,1)}, u32[]{:S(2)}) copy-start(bf16[2048,384]{1,0:T(8,128)(2,1)} %param.8) | copy-start | bytes 4718596
  100.6 3.9 %copy-start.7 = (bf16[2048,384]{1,0:T(8,128)(2,1)S(1)}, bf16[2048,384]{1,0:T(8,128)(2,1)}, u32[]{:S(2)}) copy-start(bf16[2048,384]{1,0:T(8,128)(2,1)} %get-tuple-element.23) | copy-start | bytes 4718596
Sparse Core Ops, SparseCore 0:
  18.3 31.1 all-reduce.3
  59.9 18.2 reduce-scatter.4
  86.5 25.2 reduce-scatter.2
where the time goes:
time: 121 us; the launch traced here: 120 us
  matrix products  46.6 us (39%)
  blocking collectives  22.6 us (19%)
  other arithmetic  18.3 us (15%)
  between operations  14 us (12%)
  waiting for transfers between devices  13 us (11%)
  local copies, waits for them, and re-layouts  5.42 us (4%)
    psum x1, blocking collectives, xca_local(): gram, q_sq, k_sq = lax.psum((gram_part, q_sq_part, k_sq_part), 'sp')  16.3 us
    psum x1, waiting for transfers between devices, xca_local(): gram, q_sq, k_sq = lax.psum((gram_part, q_sq_part, k_sq_part), 'sp')  9.78 us
    dot_general x1, matrix products, xca_local(): jnp.einsum('nc,dc->nd', d_qkv, w_qkv, preferred_element_type=jnp.float32)  7.91 us
    psum x1, blocking collectives, xca_local(): d_gamma, d_beta = lax.psum((d_gamma_part, d_beta_part), 'sp')  6.3 us
    dot_general x1, matrix products, xca_local(): jnp.einsum('hij,nhi->nhj', d_gram, query_h, preferred_element_type=jnp.fl...  5.43 us
    unnamed x26, local copies, waits for them, and re-layouts  5.41 us
    dot_general x1, matrix products, xca_local(): jnp.einsum('hij,nhj->nhi', d_gram, key_h, preferred_element_type=jnp.floa...  5.1 us
    dot_general x1, matrix products, xca_local(): jnp.einsum('nhi,hij->nhj', d_out_h, attn, preferred_element_type=jnp.floa...  4.32 us
  transfers between devices with their start and end apart: 3, of which 2 were waited for; matrix products, arithmetic and copies ran while one was open for 37% of the time, Pallas kernels for 0%

commit v1 on v0

v1 whole, which is shorter than its diff:
```python
import jax
import jax.numpy as jnp
from jax import lax
from jax.experimental import pallas as pl
from jax.experimental.pallas import tpu as pltpu
from jax.sharding import PartitionSpec as P

LN_EPS = 1e-6
F32 = jnp.float32
BF16 = jnp.bfloat16
N = 2048
D = 384
HD = 48
GW = 192
PW = 256
RB = 96
CH = 256
NCH = N // CH

NN = (((1,), (0,)), ((), ()))
NT = (((1,), (1,)), ((), ()))
TN = (((0,), (0,)), ((), ()))


def mm(a, b, dims):
    return lax.dot_general(a, b, dims, preferred_element_type=F32)


def kernel(x_hbm, dy_hbm, gamma, beta, w_hbm, wo_hbm, temp,
           y_out, dx_out, dw_out, dwo_out, dg_out, db_out, dt_out,
           x, dy, w, wo, wt, u, ut, qkvt, dqkvt, dot_, ot, mean_s, rstd_s, s_acc,
           pk1, pk2, ra, sb, rb, cs, rc, abd, gbd, keep, part, rd1, rd2, ls, rl, es, er,
           in_sem, x_sem, ssem, rsem):
    sp = lax.axis_index("sp")
    core = lax.rem(sp, 2)
    peer = 1 - core
    partner = sp + 1 - 2 * core
    other = lax.rem(sp + 2, 4)
    cross = lax.rem(partner + 2, 4)

    barrier = pltpu.get_barrier_semaphore()
    for dev in (partner, other):
        pl.semaphore_signal(barrier, inc=1, device_id={"sp": dev}, device_id_type=pl.DeviceIdType.MESH)

    w_copy = pltpu.make_async_copy(w_hbm, w, in_sem.at[0])
    wo_copy = pltpu.make_async_copy(wo_hbm, wo, in_sem.at[1])
    dy_copy = pltpu.make_async_copy(dy_hbm, dy, in_sem.at[2])

    def x_copy(i):
        rows = pl.ds(i * CH, CH)
        return pltpu.make_async_copy(x_hbm.at[rows], x.at[rows], x_sem.at[i])

    x_copy(0).start()
    w_copy.start()
    for i in range(1, NCH):
        x_copy(i).start()
    wo_copy.start()
    dy_copy.start()

    def send(slot, src, dst, dev):
        copy = pltpu.make_async_remote_copy(
            src_ref=src, dst_ref=dst, send_sem=ssem.at[slot], recv_sem=rsem.at[slot],
            device_id={"sp": dev}, device_id_type=pl.DeviceIdType.MESH)
        copy.start()
        return copy

    lane = lax.broadcasted_iota(jnp.int32, (HD, PW), 1)
    row = lax.broadcasted_iota(jnp.int32, (HD, PW), 0)
    heads = [(lane >= HD * h) & (lane < HD * h + HD) for h in range(4)]
    eyes = [lane == row + HD * h for h in range(4)]
    valid = lane < GW
    s_acc[...] = jnp.zeros_like(s_acc)
    pk1[...] = jnp.zeros_like(pk1)
    pk2[...] = jnp.zeros_like(pk2)

    def layer_norm(i):
        rows = pl.ds(pl.multiple_of(i * CH, CH), CH)
        xf = x[rows, :].astype(F32)
        mean = jnp.mean(xf, axis=-1, keepdims=True)
        cen = xf - mean
        rstd = lax.rsqrt(jnp.mean(cen * cen, axis=-1, keepdims=True) + LN_EPS)
        mean_s[rows, :] = mean
        rstd_s[rows, :] = rstd
        u[rows, :] = (cen * rstd * gamma[...] + beta[...]).astype(BF16)

    def qk_chunk(i):
        cols = pl.ds(pl.multiple_of(i * CH, CH), CH)
        res = mm(wt[0:2 * D, :], u[cols, :], NT).astype(BF16)
        for s in range(4):
            qkvt[s // 2, s % 2, :, cols] = res[s * GW:(s + 1) * GW]
        sq = jnp.square(res.astype(F32))
        s_acc[...] += sq[:, :128] + sq[:, 128:]

    x_copy(0).wait()
    layer_norm(0)
    w_copy.wait()
    wt[...] = w[...].T

    @pl.loop(0, NCH - 1)
    def _(i):
        rows = pl.ds(pl.multiple_of((i + 1) * CH, CH), CH)
        pltpu.make_async_copy(x_hbm.at[rows], x.at[rows], x_sem.at[i + 1]).wait()
        qk_chunk(i)
        layer_norm(i + 1)

    qk_chunk(NCH - 1)

    def compact(full):
        out = jnp.zeros((HD, GW), F32)
        for h in range(4):
            out = jnp.where(heads[h][:, :GW], full[HD * h:HD * h + HD], out)
        return out

    s_col = jnp.sum(s_acc[...], axis=-1, keepdims=True)
    for g in range(2):
        pk1[g, :, 0:GW] = compact(mm(qkvt[0, g], qkvt[1, g], NT))
        blk = pk1[g]
        for h in range(4):
            r = g * GW + h * HD
            blk = jnp.where(lane == GW + h, s_col[r:r + HD], blk)
            blk = jnp.where(lane == GW + 4 + h, s_col[D + r:D + r + HD], blk)
        pk1[g] = blk

    pl.semaphore_wait(barrier, 2)
    a1 = send(0, pk1.at[peer], ra.at[0], partner)

    CV = 512

    @pl.loop(0, N // CV)
    def _(i):
        cols = pl.ds(pl.multiple_of(i * CV, CV), CV)
        res = mm(wt[2 * D:3 * D, :], u[cols, :], NT).astype(BF16)
        qkvt[2, 0, :, cols] = res[:GW]
        qkvt[2, 1, :, cols] = res[GW:]

    a1.wait_recv()
    sb[0] = pk1[core] + ra[0]
    b1 = send(1, sb.at[0], rb.at[0], other)

    wo_copy.wait()
    dy_copy.wait()

    @pl.loop(0, N // CV)
    def _(i):
        cols = pl.ds(pl.multiple_of(i * CV, CV), CV)
        res = mm(wo[...], dy[cols, :], NT).astype(BF16)
        dot_[0, :, cols] = res[:GW]
        dot_[1, :, cols] = res[GW:]

    for g in range(2):
        pk2[g, :, 0:GW] = compact(mm(dot_[g], qkvt[2, g], NT))
    a2 = send(2, pk2.at[peer], ra.at[1], partner)

    @pl.loop(0, NCH // 2)
    def _(i):
        cols = pl.ds(pl.multiple_of(i * CH, CH), CH)
        ut[:, cols] = u[cols, :].T

    a2.wait_recv()
    sb[1] = pk2[core] + ra[1]
    b2 = send(3, sb.at[1], rb.at[1], other)

    @pl.loop(NCH // 2, NCH)
    def _(i):
        cols = pl.ds(pl.multiple_of(i * CH, CH), CH)
        ut[:, cols] = u[cols, :].T

    def seg_sum(v):
        out = jnp.zeros_like(v)
        for h in range(4):
            out = jnp.where(heads[h], jnp.sum(jnp.where(heads[h], v, 0.0), axis=-1, keepdims=True), out)
        return out

    def expand(dst, g, comp):
        for h in range(4):
            dst[g, HD * h:HD * h + HD, :] = jnp.where(heads[h], comp, 0.0)[:, :GW].astype(BF16)

    b1.wait_recv()
    gs = sb[0] + rb[0]
    rq2 = jnp.zeros((HD, PW), F32)
    rk2 = jnp.zeros((HD, PW), F32)
    tau = jnp.zeros((HD, PW), F32)
    for h in range(4):
        sq_h = jnp.sum(jnp.where(lane == GW + h, gs, 0.0), axis=-1, keepdims=True)
        sk_h = jnp.sum(jnp.where(lane == GW + 4 + h, gs, 0.0), axis=-1, keepdims=True)
        rq2 = jnp.where(heads[h], sq_h, rq2)
        rk2 = jnp.where(eyes[h], sk_h, rk2)
        tau = jnp.where(heads[h], temp[core * 4 + h], tau)
    sk2 = jnp.sum(rk2, axis=0, keepdims=True)
    q_inv = lax.rsqrt(jnp.where(valid, rq2, 1.0))
    k_inv = lax.rsqrt(jnp.where(valid, sk2, 1.0))
    gram = jnp.where(valid, gs, 0.0)
    scores = tau * gram * q_inv * k_inv
    top = jnp.zeros((HD, PW), F32)
    for h in range(4):
        top = jnp.where(heads[h], jnp.max(jnp.where(heads[h], scores, -jnp.inf), axis=-1, keepdims=True), top)
    e = jnp.where(valid, jnp.exp(scores - top), 0.0)
    prob = jnp.where(valid, e / jnp.where(valid, seg_sum(e), 1.0), 0.0)
    cs[0] = prob
    c1 = send(4, cs.at[0], rc.at[0], partner)
    keep[0] = prob
    keep[1] = scores
    keep[2] = gram * q_inv * k_inv
    keep[3] = tau * q_inv * k_inv
    keep[4] = jnp.where(valid, rq2, 1.0)
    keep[5] = jnp.where(valid, jnp.broadcast_to(sk2, (HD, PW)), 1.0)
    expand(abd, core, prob)

    def attend(g):
        ot[g] = mm(abd[g], qkvt[2, g], NN).astype(BF16)

    def d_value(g):
        dqkvt[2, g] = mm(abd[g], dot_[g], TN).astype(BF16)

    attend(core)
    d_value(core)
    c1.wait_recv()
    expand(abd, peer, rc[0])
    attend(peer)

    def all_rows(ref):
        return ref[...].reshape(D, N)

    def weight_send(t):
        return (send(6 + 3 * t, part.at[t, cross], rd1.at[t], partner),
                send(7 + 3 * t, part.at[t, partner], rd2.at[t], partner))

    def link_send(t, first):
        first.wait_recv()
        ls[t] = part[t, other] + rd1[t]
        return send(8 + 3 * t, ls.at[t], rl.at[t], other)

    part[0] = mm(all_rows(ot), dy[...], NN).reshape(4, RB, D)
    d0 = weight_send(0)

    b2.wait_recv()
    da = jnp.where(valid, (sb[1] + rb[1]).astype(BF16).astype(F32), 0.0)
    p = keep[0]
    ds = p * (da - seg_sum(da * p))
    weighted = ds * keep[1]
    dtemp = seg_sum(ds * keep[2])
    dtemp = jnp.sum(dtemp, axis=0, keepdims=True)
    dgram = (ds * keep[3]).astype(BF16).astype(F32)
    dsq = -seg_sum(weighted) / keep[4]
    dsk = -jnp.sum(weighted, axis=0, keepdims=True) / keep[5]
    blk = dgram
    for h in range(4):
        dsk_h = jnp.sum(jnp.where(eyes[h], dsk, 0.0), axis=-1, keepdims=True)
        dsq_h = jnp.sum(jnp.where(eyes[h], dsq, 0.0), axis=-1, keepdims=True)
        dt_h = jnp.sum(jnp.where(lane == HD * h, dtemp, 0.0), axis=-1, keepdims=True)
        blk = jnp.where(lane == GW + h, dsq_h, blk)
        blk = jnp.where(lane == GW + 4 + h, dsk_h, blk)
        blk = jnp.where(lane == GW + 8 + h, dt_h, blk)
    cs[1] = blk
    c2 = send(5, cs.at[1], rc.at[1], partner)

    l0 = link_send(0, d0[0])

    d_value(peer)
    part[1] = mm(all_rows(ut), dqkvt[2].reshape(D, N), NT).reshape(4, RB, D)
    d1 = weight_send(1)

    def d_qk(g, blk):
        expand(gbd, g, jnp.where(valid, blk, 0.0))
        cols = []
        for b in (GW, GW + 4):
            cols.append(jnp.concatenate(
                [jnp.sum(jnp.where(lane == b + h, blk, 0.0), axis=-1, keepdims=True) for h in range(4)], axis=0))
        dqkvt[0, g] = (mm(gbd[g], qkvt[1, g], NN) + qkvt[0, g].astype(F32) * cols[0]).astype(BF16)
        dqkvt[1, g] = (mm(gbd[g], qkvt[0, g], TN) + qkvt[1, g].astype(F32) * cols[1]).astype(BF16)

    d_qk(core, cs[1])
    c2.wait_recv()
    d_qk(peer, rc[1])
    l1 = link_send(1, d1[0])
    part[2] = mm(ut[...], dqkvt[1].reshape(D, N), NT).reshape(4, RB, D)
    d2 = weight_send(2)
    part[3] = mm(ut[...], dqkvt[0].reshape(D, N), NT).reshape(4, RB, D)
    d3 = weight_send(3)
    l2 = link_send(2, d2[0])
    l3 = link_send(3, d3[0])

    lane8 = lax.broadcasted_iota(jnp.int32, (1, 8), 1)
    dt = jnp.zeros((1, 8), F32)
    for g, src in ((core, cs), (peer, rc)):
        head_row = src[1][0:1, :]
        for h in range(4):
            val = jnp.sum(jnp.where(lane[0:1] == GW + 8 + h, head_row, 0.0), axis=-1, keepdims=True)
            dt = jnp.where(lane8 == g * 4 + h, val, dt)
    dt_out[...] = dt

    es[...] = jnp.zeros_like(es)

    @pl.loop(0, NCH)
    def _(i):
        rows = pl.ds(pl.multiple_of(i * CH, CH), CH)
        proj = mm(ot[:, :, rows].reshape(D, CH), wo[...], TN)
        xf = x[rows, :].astype(F32)
        y_out[rows, :] = (xf + proj).astype(BF16)
        dut = mm(w[...], dqkvt[:, :, :, rows].reshape(3 * D, CH), NN).astype(BF16)
        du = dut.T.astype(F32)
        rstd = rstd_s[rows, :]
        xhat = (xf - mean_s[rows, :]) * rstd
        es[0:1, :] += jnp.sum(du * xhat, axis=0, keepdims=True)
        es[1:2, :] += jnp.sum(du, axis=0, keepdims=True)
        dh = du * gamma[...]
        m1 = jnp.mean(dh, axis=-1, keepdims=True)
        m2 = jnp.mean(dh * xhat, axis=-1, keepdims=True)
        dx_out[rows, :] = (dy[rows, :].astype(F32) + rstd * (dh - m1 - xhat * m2)).astype(BF16)

    e1 = send(18, es, er.at[0], partner)
    e1.wait()
    er[1] = es[...] + er[0]
    e2 = send(19, er.at[1], er.at[2], other)

    outs = ((dwo_out, slice(0, D)), (dw_out, slice(2 * D, 3 * D)), (dw_out, slice(D, 2 * D)), (dw_out, slice(0, D)))
    for t, (d, l) in enumerate(((d0, l0), (d1, l1), (d2, l2))):
        d[1].wait_recv()
        l.wait_recv()
        outs[t][0][:, outs[t][1]] = (part[t, sp] + rd2[t] + rl[t]).astype(BF16)
    e2.wait()
    tot = er[1] + er[2]
    dg_out[...] = tot[0:1]
    db_out[...] = tot[1:2]
    d3[1].wait_recv()
    l3.wait_recv()
    outs[3][0][:, outs[3][1]] = (part[3, sp] + rd2[3] + rl[3]).astype(BF16)
    for copy in (a1, a2, b1, b2, c1, c2, *d0, *d1, *d2, *d3, l0, l1, l2, l3):
        copy.wait_send()


def local_step(x_rows, dy_rows, ln_gamma, ln_beta, w_qkv, w_out, temperature):
    any_spec = pl.BlockSpec(memory_space=pl.ANY)
    vmem = pl.BlockSpec(memory_space=pltpu.VMEM)
    smem = pl.BlockSpec(memory_space=pltpu.SMEM)
    sds = jax.ShapeDtypeStruct
    outs = pl.pallas_call(
        kernel,
        out_shape=(sds((N, D), BF16), sds((N, D), BF16), sds((RB, 3 * D), BF16), sds((RB, D), BF16),
                   sds((1, D), F32), sds((1, D), F32), sds((1, 8), F32)),
        in_specs=[any_spec, any_spec, vmem, vmem, any_spec, any_spec, smem],
        out_specs=(vmem,) * 7,
        scratch_shapes=[
            pltpu.VMEM((N, D), BF16),
            pltpu.VMEM((N, D), BF16),
            pltpu.VMEM((D, 3 * D), BF16),
            pltpu.VMEM((D, D), BF16),
            pltpu.VMEM((3 * D, D), BF16),
            pltpu.VMEM((N, D), BF16),
            pltpu.VMEM((D, N), BF16),
            pltpu.VMEM((3, 2, GW, N), BF16),
            pltpu.VMEM((3, 2, GW, N), BF16),
            pltpu.VMEM((2, GW, N), BF16),
            pltpu.VMEM((2, GW, N), BF16),
            pltpu.VMEM((N, 1), F32),
            pltpu.VMEM((N, 1), F32),
            pltpu.VMEM((2 * D, 128), F32),
            pltpu.VMEM((2, HD, PW), F32),
            pltpu.VMEM((2, HD, PW), F32),
            pltpu.VMEM((2, HD, PW), F32),
            pltpu.VMEM((2, HD, PW), F32),
            pltpu.VMEM((2, HD, PW), F32),
            pltpu.VMEM((2, HD, PW), F32),
            pltpu.VMEM((2, HD, PW), F32),
            pltpu.VMEM((2, GW, GW), BF16),
            pltpu.VMEM((2, GW, GW), BF16),
            pltpu.VMEM((6, HD, PW), F32),
            pltpu.VMEM((4, 4, RB, D), F32),
            pltpu.VMEM((4, RB, D), F32),
            pltpu.VMEM((4, RB, D), F32),
            pltpu.VMEM((4, RB, D), F32),
            pltpu.VMEM((4, RB, D), F32),
            pltpu.VMEM((8, D), F32),
            pltpu.VMEM((3, 8, D), F32),
            pltpu.SemaphoreType.DMA((3,)),
            pltpu.SemaphoreType.DMA((NCH,)),
            pltpu.SemaphoreType.DMA((20,)),
            pltpu.SemaphoreType.DMA((20,)),
        ],
        compiler_params=pltpu.CompilerParams(collective_id=0, has_side_effects=True, vmem_limit_bytes=48 << 20),
        name="xca",
    )(x_rows, dy_rows, ln_gamma.reshape(1, D), ln_beta.reshape(1, D), w_qkv, w_out, temperature)
    y, dx, dw, dwo, dg, db, dt = outs
    return y, dx, dw, dwo, dg.reshape(D), db.reshape(D), dt.reshape(8)


def solution(mesh):
    row_spec = P(('dp', 'sp'), None)
    full_mat = P(None, None)
    full_vec = P(None)
    part_vec = P('dp')
    return jax.shard_map(local_step, mesh=mesh,
                         in_specs=(row_spec, row_spec, full_vec, full_vec, full_mat, full_mat, full_vec),
                         out_specs=(row_spec, row_spec, row_spec, row_spec, part_vec, part_vec, part_vec),
                         check_vma=False)
```

time: 121 us -> 46.8 us (0.39)
  matrix products: 46.6 us -> 0 us
  Pallas kernels: 0 us -> 35 us
  blocking collectives: 22.6 us -> 0 us
  other arithmetic: 18.3 us -> 1.19 us
  between operations: 14 us -> 0.65 us
  waiting for transfers between devices: 13 us -> 0 us
  local copies, waits for them, and re-layouts: 5.42 us -> 9.67 us
    dot_general x12 -> x0, matrix products: 46.6 us -> none  [the longest x1 7.91 us: xca_local(): jnp.einsum('nc,dc->nd', d_qkv, w_qkv, preferred_element_type=jnp.float32)]
    pallas_call x0 -> x1, Pallas kernels: none -> 35 us  [local_step(): pl.pallas_call(kernel, out_shape=(sds((N, D), BF16), sds((N, D), BF16), s...]
    psum x2 -> x0, blocking collectives: 22.6 us -> none  [the longest x1 16.3 us: xca_local(): gram, q_sq, k_sq = lax.psum((gram_part, q_sq_part, k_sq_part), 'sp')]
    psum x1 -> x0, waiting for transfers between devices: 9.78 us -> none  [xca_local(): gram, q_sq, k_sq = lax.psum((gram_part, q_sq_part, k_sq_part), 'sp')]
    convert_element_type x3 -> x0, other arithmetic: 5.92 us -> none  [the longest x1 2.64 us: xca_local(): dx_rows = (dy_rows.astype(jnp.float32) + d_ln).astype(jnp.bfloat16)]
    sub x2 -> x0, other arithmetic: 4.96 us -> none  [the longest x1 2.63 us: state_softmax_bwd(): d_attn - jnp.sum(d_attn * attn_f32, axis=-1, keepdims=True)]
    reduce_sum x3 -> x0, other arithmetic: 4.79 us -> none  [the longest x1 2.2 us: layer_norm_fwd(): jnp.mean(centered * centered, axis=-1, keepdims=True) + LN_EPS]
    reduce_scatter x2 -> x0, waiting for transfers between devices: 3.14 us -> none  [the longest x1 3.14 us: xca_local(): lax.psum_scatter(dw_qkv_part, 'sp', scatter_dimension=0, tiled=True)]
  transfers between devices with their start and end apart: 3 -> 0, of which waited for: 2 -> 0; matrix products, arithmetic and copies ran while one was open for 37% -> 0% of each run, Pallas kernels for 0% -> 0%
where the time goes in v1:
time: 46.8 us; the launch traced here: 46.5 us
  Pallas kernels  35 us (75%)
  local copies, waits for them, and re-layouts  9.67 us (21%)
  other arithmetic  1.19 us (3%)
  between operations  0.65 us (1%)
    pallas_call x1, Pallas kernels, local_step(): pl.pallas_call(kernel, out_shape=(sds((N, D), BF16), sds((N, D), BF16), s...  35 us
    unnamed x13, local copies, waits for them, and re-layouts  8.3 us
    pallas_call x2, other arithmetic, local_step(): pl.pallas_call(kernel, out_shape=(sds((N, D), BF16), sds((N, D), BF16), s...  1.19 us

profile of v1, /device:TPU:0, one launch (start us, length us, event | category | flops | bytes accessed | tf_op | source)
XLA Modules:
  0.0 46.5 jit_solution(5921985700879103178)
XLA Ops:
  0.6 0.7 %reshape.29.gamma = f32[1,384]{1,0:T(1,128)S(1)} reshape(f32[384]{0:T(512)} %param.9) | data formatting | bytes 3072 | tf_op jit(solution)/shard_map/reshape | solution.py:382
  1.3 0.7 %reshape.30.beta = f32[1,384]{1,0:T(1,128)S(1)} reshape(f32[384]{0:T(512)} %param.10) | data formatting | bytes 3072 | tf_op jit(solution)/shard_map/reshape | solution.py:382
  2.0 0.0 copy-start
  2.0 1.4 %copy-done = bf16[2048,384]{1,0:T(8,128)(2,1)S(1)} copy-done((bf16[2048,384]{1,0:T(8,128)(2,1)S(1)}, bf16[2048,384]{1,0:T(8,128)(2,1)}, u32[]{:S(2)}) %copy-start) | copy-done | bytes 1572888
  3.4 0.0 copy-start.1
  3.4 1.2 %copy-done.1 = bf16[384,1152]{1,0:T(8,128)(2,1)S(1)} copy-done((bf16[384,1152]{1,0:T(8,128)(2,1)S(1)}, bf16[384,1152]{1,0:T(8,128)(2,1)}, u32[]{:S(2)}) %copy-start.1) | copy-done | bytes 884760
  4.6 0.0 copy-start.2
  4.6 1.0 %copy-done.2 = bf16[384,384]{1,0:T(8,128)(2,1)S(1)} copy-done((bf16[384,384]{1,0:T(8,128)(2,1)S(1)}, bf16[384,384]{1,0:T(8,128)(2,1)}, u32[]{:S(2)}) %copy-start.2) | copy-done | bytes 294936
  5.5 0.0 copy-start.3
  5.5 0.7 %copy-done.3 = f32[8]{0:T(128)S(1)} copy-done((f32[8]{0:T(128)S(1)}, f32[8]{0:T(128)}, u32[]{:S(2)}) %copy-start.3) | copy-done | bytes 56
  6.2 35.0 %xca.1 = (bf16[2048,384]{1,0:T(8,128)(2,1)S(1)}, bf16[2048,384]{1,0:T(8,128)(2,1)S(1)}, bf16[96,1152]{1,0:T(8,128)(2,1)S(1)}, bf16[96,384]{1,0:T(8,128)(2,1)S(1)...) custom-call(bf16[2048,384]{1,0:T(8,128)(2,1)S(1)} %copy-done, bf16[2048,384]{1,0:T(8,128)(2,1)} %dy_hbm.1, ...), custom_call_target="tpu_custom_call" | custom-call | tf_op jit(solution)/shard_map/xca/pallas_call | solution.py:337
  41.2 0.6 %reduce = f32[384]{0:T(512)} reduce(f32[1,384]{1,0:T(1,128)S(1)} %get-tuple-element.18, f32[]{:T(128)} %constant), dimensions={0}, to_apply=%get-tuple-element.18.reduce_sub_computation | reduce | bytes 3076 | tf_op jit(solution)/shard_map/xca/pallas_call | solution.py:337
  41.8 0.6 %reduce.1 = f32[384]{0:T(512)} reduce(f32[1,384]{1,0:T(1,128)S(1)} %get-tuple-element.19, f32[]{:T(128)} %constant), dimensions={0}, to_apply=%get-tuple-element.19.reduce_sub_computation | reduce | bytes 3076 | tf_op jit(solution)/shard_map/xca/pallas_call | solution.py:337
  42.4 1.1 %copy.19 = bf16[2048,384]{1,0:T(8,128)(2,1)} copy(bf16[2048,384]{1,0:T(8,128)(2,1)S(1)} %get-tuple-element.28) | data formatting | bytes 3145728
  43.5 1.1 %copy.20 = bf16[2048,384]{1,0:T(8,128)(2,1)} copy(bf16[2048,384]{1,0:T(8,128)(2,1)S(1)} %get-tuple-element.29) | data formatting | bytes 3145728
  44.7 0.7 %copy.21 = bf16[96,1152]{1,0:T(8,128)(2,1)} copy(bf16[96,1152]{1,0:T(8,128)(2,1)S(1)} %get-tuple-element.30) | data formatting | bytes 442368
  45.4 0.6 %copy.22 = bf16[96,384]{1,0:T(8,128)(2,1)} copy(bf16[96,384]{1,0:T(8,128)(2,1)S(1)} %get-tuple-element.31) | data formatting | bytes 147456
  46.0 0.5 %copy.23 = f32[8]{0:T(128)} copy(f32[8]{0:T(128)S(1)} %bitcast.1) | data formatting | bytes 64
Async XLA Ops:
  2.0 1.4 %copy-start = (bf16[2048,384]{1,0:T(8,128)(2,1)S(1)}, bf16[2048,384]{1,0:T(8,128)(2,1)}, u32[]{:S(2)}) copy-start(bf16[2048,384]{1,0:T(8,128)(2,1)} %x_hbm.1) | copy-start | bytes 4718596
  3.4 1.2 %copy-start.1 = (bf16[384,1152]{1,0:T(8,128)(2,1)S(1)}, bf16[384,1152]{1,0:T(8,128)(2,1)}, u32[]{:S(2)}) copy-start(bf16[384,1152]{1,0:T(8,128)(2,1)} %w_hbm.1) | copy-start | bytes 2654212
  4.6 1.0 %copy-start.2 = (bf16[384,384]{1,0:T(8,128)(2,1)S(1)}, bf16[384,384]{1,0:T(8,128)(2,1)}, u32[]{:S(2)}) copy-start(bf16[384,384]{1,0:T(8,128)(2,1)} %wo_hbm.1) | copy-start | bytes 884740
  5.5 0.7 %copy-start.3 = (f32[8]{0:T(128)S(1)}, f32[8]{0:T(128)}, u32[]{:S(2)}) copy-start(f32[8]{0:T(128)} %temp.1) | copy-start | bytes 100

commit v2 on v1

--- a/solution.py
+++ b/solution.py
@@ -26,11 +26,11 @@
     return lax.dot_general(a, b, dims, preferred_element_type=F32)
 
 
-def kernel(x_hbm, dy_hbm, gamma, beta, w_hbm, wo_hbm, temp,
+def kernel(x_hbm, dy_hbm, gamma_hbm, beta_hbm, w_hbm, wo_hbm, temp_hbm,
            y_out, dx_out, dw_out, dwo_out, dg_out, db_out, dt_out,
            x, dy, w, wo, wt, u, ut, qkvt, dqkvt, dot_, ot, mean_s, rstd_s, s_acc,
            pk1, pk2, ra, sb, rb, cs, rc, abd, gbd, keep, part, rd1, rd2, ls, rl, es, er,
-           in_sem, x_sem, ssem, rsem):
+           gamma, beta, temp, in_sem, x_sem, ssem, rsem):
     sp = lax.axis_index("sp")
     core = lax.rem(sp, 2)
     peer = 1 - core
@@ -45,17 +45,23 @@
     w_copy = pltpu.make_async_copy(w_hbm, w, in_sem.at[0])
     wo_copy = pltpu.make_async_copy(wo_hbm, wo, in_sem.at[1])
     dy_copy = pltpu.make_async_copy(dy_hbm, dy, in_sem.at[2])
+    gamma_copy = pltpu.make_async_copy(gamma_hbm, gamma.at[0], in_sem.at[3])
+    beta_copy = pltpu.make_async_copy(beta_hbm, beta.at[0], in_sem.at[4])
+    temp_copy = pltpu.make_async_copy(temp_hbm, temp, in_sem.at[5])
 
     def x_copy(i):
         rows = pl.ds(i * CH, CH)
         return pltpu.make_async_copy(x_hbm.at[rows], x.at[rows], x_sem.at[i])
 
     x_copy(0).start()
+    gamma_copy.start()
+    beta_copy.start()
     w_copy.start()
     for i in range(1, NCH):
         x_copy(i).start()
     wo_copy.start()
     dy_copy.start()
+    temp_copy.start()
 
     def send(slot, src, dst, dev):
         copy = pltpu.make_async_remote_copy(
@@ -91,6 +97,8 @@
         sq = jnp.square(res.astype(F32))
         s_acc[...] += sq[:, :128] + sq[:, 128:]
 
+    gamma_copy.wait()
+    beta_copy.wait()
     x_copy(0).wait()
     layer_norm(0)
     w_copy.wait()
@@ -139,6 +147,7 @@
 
     wo_copy.wait()
     dy_copy.wait()
+    temp_copy.wait()
 
     @pl.loop(0, N // CV)
     def _(i):
@@ -329,16 +338,24 @@
         copy.wait_send()
 
 
+def write_out(y, dx, dw, dwo, dg, db, dt, y_o, dx_o, dw_o, dwo_o, dg_o, db_o, dt_o, sem):
+    copies = [pltpu.make_async_copy(src, dst, sem.at[i]) for i, (src, dst) in enumerate(
+        ((y, y_o), (dx, dx_o), (dw, dw_o), (dwo, dwo_o), (dg.at[0], dg_o), (db.at[0], db_o), (dt.at[0], dt_o)))]
+    for copy in copies:
+        copy.start()
+    for copy in copies:
+        copy.wait()
+
+
 def local_step(x_rows, dy_rows, ln_gamma, ln_beta, w_qkv, w_out, temperature):
-    any_spec = pl.BlockSpec(memory_space=pl.ANY)
+    hbm = pl.BlockSpec(memory_space=pltpu.HBM)
     vmem = pl.BlockSpec(memory_space=pltpu.VMEM)
-    smem = pl.BlockSpec(memory_space=pltpu.SMEM)
     sds = jax.ShapeDtypeStruct
     outs = pl.pallas_call(
         kernel,
         out_shape=(sds((N, D), BF16), sds((N, D), BF16), sds((RB, 3 * D), BF16), sds((RB, D), BF16),
                    sds((1, D), F32), sds((1, D), F32), sds((1, 8), F32)),
-        in_specs=[any_spec, any_spec, vmem, vmem, any_spec, any_spec, smem],
+        in_specs=[hbm] * 7,
         out_specs=(vmem,) * 7,
         scratch_shapes=[
             pltpu.VMEM((N, D), BF16),
@@ -372,16 +389,26 @@
             pltpu.VMEM((4, RB, D), F32),
             pltpu.VMEM((8, D), F32),
             pltpu.VMEM((3, 8, D), F32),
-            pltpu.SemaphoreType.DMA((3,)),
+            pltpu.VMEM((1, D), F32),
+            pltpu.VMEM((1, D), F32),
+            pltpu.SMEM((8,), F32),
+            pltpu.SemaphoreType.DMA((6,)),
             pltpu.SemaphoreType.DMA((NCH,)),
             pltpu.SemaphoreType.DMA((20,)),
             pltpu.SemaphoreType.DMA((20,)),
         ],
         compiler_params=pltpu.CompilerParams(collective_id=0, has_side_effects=True, vmem_limit_bytes=48 << 20),
         name="xca",
-    )(x_rows, dy_rows, ln_gamma.reshape(1, D), ln_beta.reshape(1, D), w_qkv, w_out, temperature)
-    y, dx, dw, dwo, dg, db, dt = outs
-    return y, dx, dw, dwo, dg.reshape(D), db.reshape(D), dt.reshape(8)
+    )(x_rows, dy_rows, ln_gamma, ln_beta, w_qkv, w_out, temperature)
+    return pl.pallas_call(
+        write_out,
+        out_shape=(sds((N, D), BF16), sds((N, D), BF16), sds((RB, 3 * D), BF16), sds((RB, D), BF16),
+                   sds((D,), F32), sds((D,), F32), sds((8,), F32)),
+        in_specs=[vmem] * 7,
+        out_specs=(hbm,) * 7,
+        scratch_shapes=[pltpu.SemaphoreType.DMA((7,))],
+        name="write_out",
+    )(*outs)
 
 
 def solution(mesh):

time: 46.8 us -> 50 us (1.068)
  Pallas kernels: 35 us -> 38.2 us
  other arithmetic: 1.19 us -> 0 us
  local copies, waits for them, and re-layouts: 9.67 us -> 10.8 us
    pallas_call x0 -> x1, Pallas kernels: none -> 3.72 us  [local_step(): pl.pallas_call(write_out, out_shape=(sds((N, D), BF16), sds((N, D), BF16)...]
    unnamed x13 -> x26, local copies, waits for them, and re-layouts: 8.3 us -> 10.8 us
    reshape x2 -> x0, local copies, waits for them, and re-layouts: 1.37 us -> none  [the longest x1 0.68 us: local_step(): ln_gamma.reshape(1, D)]
    pallas_call x2 -> x0, other arithmetic: 1.19 us -> none  [local_step(): pl.pallas_call(kernel, out_shape=(sds((N, D), BF16), sds((N, D), BF16), s...]
where the time goes in v2:
time: 50 us; the launch traced here: 49.7 us
  Pallas kernels  38.2 us (76%)
  local copies, waits for them, and re-layouts  10.8 us (22%)
  between operations  0.67 us (1%)
    pallas_call x1, Pallas kernels, local_step(): pl.pallas_call(kernel, out_shape=(sds((N, D), BF16), sds((N, D), BF16), s...  34.5 us
    unnamed x26, local copies, waits for them, and re-layouts  10.8 us
    pallas_call x1, Pallas kernels, local_step(): pl.pallas_call(write_out, out_shape=(sds((N, D), BF16), sds((N, D), BF16)...  3.72 us

profile of v2, /device:TPU:0, one launch (start us, length us, event | category | flops | bytes accessed | tf_op | source)
XLA Modules:
  0.0 49.7 jit_solution(18210137037585456865)
XLA Ops:
  0.6 0.0 copy-start.2
  0.6 1.4 %copy-done.2 = bf16[2048,384]{1,0:T(8,128)(2,1)S(1)} copy-done((bf16[2048,384]{1,0:T(8,128)(2,1)S(1)}, bf16[2048,384]{1,0:T(8,128)(2,1)}, u32[]{:S(2)}) %copy-start.2) | copy-done | bytes 1572888
  2.0 0.0 copy-start.3
  2.0 1.2 %copy-done.3 = bf16[384,1152]{1,0:T(8,128)(2,1)S(1)} copy-done((bf16[384,1152]{1,0:T(8,128)(2,1)S(1)}, bf16[384,1152]{1,0:T(8,128)(2,1)}, u32[]{:S(2)}) %copy-start.3) | copy-done | bytes 884760
  3.2 0.0 copy-start.4
  3.2 1.0 %copy-done.4 = bf16[384,384]{1,0:T(8,128)(2,1)S(1)} copy-done((bf16[384,384]{1,0:T(8,128)(2,1)S(1)}, bf16[384,384]{1,0:T(8,128)(2,1)}, u32[]{:S(2)}) %copy-start.4) | copy-done | bytes 294936
  4.2 0.0 copy-start.7
  4.2 0.7 %copy-done.7 = f32[384]{0:T(512)S(1)} copy-done((f32[384]{0:T(512)S(1)}, f32[384]{0:T(512)}, u32[]{:S(2)}) %copy-start.7) | copy-done | bytes 1560
  4.9 0.0 copy-start.8
  4.9 0.7 %copy-done.8 = f32[384]{0:T(512)S(1)} copy-done((f32[384]{0:T(512)S(1)}, f32[384]{0:T(512)}, u32[]{:S(2)}) %copy-start.8) | copy-done | bytes 1560
  5.5 0.0 copy-start.12
  5.5 0.7 %copy-done.12 = f32[8]{0:T(128)S(1)} copy-done((f32[8]{0:T(128)S(1)}, f32[8]{0:T(128)}, u32[]{:S(2)}) %copy-start.12) | copy-done | bytes 56
  6.2 34.5 %xca.1 = (bf16[2048,384]{1,0:T(8,128)(2,1)S(1)}, bf16[2048,384]{1,0:T(8,128)(2,1)S(1)}, bf16[96,1152]{1,0:T(8,128)(2,1)S(1)}, bf16[96,384]{1,0:T(8,128)(2,1)S(1)...) custom-call(bf16[2048,384]{1,0:T(8,128)(2,1)S(1)} %copy-done.2, bf16[2048,384]{1,0:T(8,128)(2,1)} %dy_hbm.1, ...), custom_call_target="tpu_custom_call" | custom-call | tf_op jit(solution)/shard_map/xca/pallas_call | solution.py:354
  40.7 0.0 copy-start
  40.7 1.2 %copy-done = bf16[2048,384]{1,0:T(8,128)(2,1)} copy-done((bf16[2048,384]{1,0:T(8,128)(2,1)}, bf16[2048,384]{1,0:T(8,128)(2,1)S(1)}, u32[]{:S(2)}) %copy-start) | copy-done | bytes 1572888
  41.9 0.0 copy-start.1
  41.9 1.1 %copy-done.1 = bf16[2048,384]{1,0:T(8,128)(2,1)} copy-done((bf16[2048,384]{1,0:T(8,128)(2,1)}, bf16[2048,384]{1,0:T(8,128)(2,1)S(1)}, u32[]{:S(2)}) %copy-start.1) | copy-done | bytes 1572888
  43.0 0.0 copy-start.5
  43.0 0.7 %copy-done.5 = bf16[96,1152]{1,0:T(8,128)(2,1)} copy-done((bf16[96,1152]{1,0:T(8,128)(2,1)}, bf16[96,1152]{1,0:T(8,128)(2,1)S(1)}, u32[]{:S(2)}) %copy-start.5) | copy-done | bytes 221208
  43.7 0.6 %copy-done.6 = bf16[96,384]{1,0:T(8,128)(2,1)} copy-done((bf16[96,384]{1,0:T(8,128)(2,1)}, bf16[96,384]{1,0:T(8,128)(2,1)S(1)}, u32[]{:S(2)}) %copy-start.6) | copy-done | bytes 73752
  44.3 0.6 %copy-done.9 = f32[1,384]{1,0:T(1,128)} copy-done((f32[1,384]{1,0:T(1,128)}, f32[1,384]{1,0:T(1,128)S(1)}, u32[]{:S(2)}) %copy-start.9) | copy-done | bytes 1560
  44.9 0.6 %copy-done.10 = f32[1,384]{1,0:T(1,128)} copy-done((f32[1,384]{1,0:T(1,128)}, f32[1,384]{1,0:T(1,128)S(1)}, u32[]{:S(2)}) %copy-start.10) | copy-done | bytes 1560
  45.5 0.5 %copy-done.11 = f32[1,8]{1,0:T(1,128)} copy-done((f32[1,8]{1,0:T(1,128)}, f32[1,8]{1,0:T(1,128)S(1)}, u32[]{:S(2)}) %copy-start.11) | copy-done | bytes 56
  46.0 3.7 %write_out.1 = (bf16[2048,384]{1,0:T(8,128)(2,1)}, bf16[2048,384]{1,0:T(8,128)(2,1)}, bf16[96,1152]{1,0:T(8,128)(2,1)}, bf16[96,384]{1,0:T(8,128)(2,1)}, f32[384]{0:T(512)}, /*index=5*/f32[384]{0:T(512)}, f32[8]{0:T(128)}) custom-call(bf16[2048,384]{1,0:T(8,128)(2,1)} %copy-done, bf16[2048,384]{1,0:T(8,128)(2,1)} %copy-done.1, bf16[96,1152]{1,0:T(8,128)(2,1)} %copy-done.5, ...), custom_call_target="tpu_custom_call" | custom-call | tf_op jit(solution)/shard_map/write_out/pallas_call | solution.py:403
  (4 shorter events, 0.0 us)
Async XLA Ops:
  0.6 1.4 %copy-start.2 = (bf16[2048,384]{1,0:T(8,128)(2,1)S(1)}, bf16[2048,384]{1,0:T(8,128)(2,1)}, u32[]{:S(2)}) copy-start(bf16[2048,384]{1,0:T(8,128)(2,1)} %x_hbm.1) | copy-start | bytes 4718596
  2.0 1.2 %copy-start.3 = (bf16[384,1152]{1,0:T(8,128)(2,1)S(1)}, bf16[384,1152]{1,0:T(8,128)(2,1)}, u32[]{:S(2)}) copy-start(bf16[384,1152]{1,0:T(8,128)(2,1)} %w_hbm.1) | copy-start | bytes 2654212
  3.2 1.0 %copy-start.4 = (bf16[384,384]{1,0:T(8,128)(2,1)S(1)}, bf16[384,384]{1,0:T(8,128)(2,1)}, u32[]{:S(2)}) copy-start(bf16[384,384]{1,0:T(8,128)(2,1)} %wo_hbm.1) | copy-start | bytes 884740
  4.2 0.7 %copy-start.7 = (f32[384]{0:T(512)S(1)}, f32[384]{0:T(512)}, u32[]{:S(2)}) copy-start(f32[384]{0:T(512)} %gamma_hbm.1) | copy-start | bytes 4612
  4.9 0.7 %copy-start.8 = (f32[384]{0:T(512)S(1)}, f32[384]{0:T(512)}, u32[]{:S(2)}) copy-start(f32[384]{0:T(512)} %beta_hbm.1) | copy-start | bytes 4612
  5.5 0.7 %copy-start.12 = (f32[8]{0:T(128)S(1)}, f32[8]{0:T(128)}, u32[]{:S(2)}) copy-start(f32[8]{0:T(128)} %temp_hbm.1) | copy-start | bytes 100
  40.7 1.2 %copy-start = (bf16[2048,384]{1,0:T(8,128)(2,1)}, bf16[2048,384]{1,0:T(8,128)(2,1)S(1)}, u32[]{:S(2)}) copy-start(bf16[2048,384]{1,0:T(8,128)(2,1)S(1)} %get-tuple-element.14.y) | copy-start | bytes 4718596
  41.9 1.1 %copy-start.1 = (bf16[2048,384]{1,0:T(8,128)(2,1)}, bf16[2048,384]{1,0:T(8,128)(2,1)S(1)}, u32[]{:S(2)}) copy-start(bf16[2048,384]{1,0:T(8,128)(2,1)S(1)} %get-tuple-element.15.dx) | copy-start | bytes 4718596
  43.0 0.7 %copy-start.5 = (bf16[96,1152]{1,0:T(8,128)(2,1)}, bf16[96,1152]{1,0:T(8,128)(2,1)S(1)}, u32[]{:S(2)}) copy-start(bf16[96,1152]{1,0:T(8,128)(2,1)S(1)} %get-tuple-element.16.dw) | copy-start | bytes 663556
  43.7 0.6 %copy-start.6 = (bf16[96,384]{1,0:T(8,128)(2,1)}, bf16[96,384]{1,0:T(8,128)(2,1)S(1)}, u32[]{:S(2)}) copy-start(bf16[96,384]{1,0:T(8,128)(2,1)S(1)} %get-tuple-element.17.dwo) | copy-start | bytes 221188
  44.3 0.6 %copy-start.9 = (f32[1,384]{1,0:T(1,128)}, f32[1,384]{1,0:T(1,128)S(1)}, u32[]{:S(2)}) copy-start(f32[1,384]{1,0:T(1,128)S(1)} %get-tuple-element.18.dg) | copy-start | bytes 4612
  44.9 0.6 %copy-start.10 = (f32[1,384]{1,0:T(1,128)}, f32[1,384]{1,0:T(1,128)S(1)}, u32[]{:S(2)}) copy-start(f32[1,384]{1,0:T(1,128)S(1)} %get-tuple-element.19.db) | copy-start | bytes 4612
  45.5 0.5 %copy-start.11 = (f32[1,8]{1,0:T(1,128)}, f32[1,8]{1,0:T(1,128)S(1)}, u32[]{:S(2)}) copy-start(f32[1,8]{1,0:T(1,128)S(1)} %get-tuple-element.20.dt) | copy-start | bytes 100

commit v3 on v2

--- a/solution.py
+++ b/solution.py
@@ -399,14 +399,16 @@
         ],
         compiler_params=pltpu.CompilerParams(collective_id=0, has_side_effects=True, vmem_limit_bytes=48 << 20),
         name="xca",
-    )(x_rows, dy_rows, ln_gamma, ln_beta, w_qkv, w_out, temperature)
+    )(*(pltpu.with_memory_space_constraint(a, pltpu.HBM)
+        for a in (x_rows, dy_rows, ln_gamma, ln_beta, w_qkv, w_out, temperature)))
     return pl.pallas_call(
         write_out,
         out_shape=(sds((N, D), BF16), sds((N, D), BF16), sds((RB, 3 * D), BF16), sds((RB, D), BF16),
                    sds((D,), F32), sds((D,), F32), sds((8,), F32)),
-        in_specs=[vmem] * 7,
+        in_specs=[pl.BlockSpec(memory_space=pl.ANY)] * 7,
         out_specs=(hbm,) * 7,
         scratch_shapes=[pltpu.SemaphoreType.DMA((7,))],
+        compiler_params=pltpu.CompilerParams(vmem_limit_bytes=1 << 20),
         name="write_out",
     )(*outs)
 

time: 50 us -> 36.1 us (0.72)
  local copies, waits for them, and re-layouts: 10.8 us -> 0 us
  Pallas kernels: 38.2 us -> 35.4 us
    unnamed x26 -> x0, local copies, waits for them, and re-layouts: 10.8 us -> none
    pallas_call x1, Pallas kernels: 3.72 us -> 1.81 us  [local_step(): pl.pallas_call(write_out, out_shape=(sds((N, D), BF16), sds((N, D), BF16)...]
    pallas_call x1, Pallas kernels: 34.5 us -> 33.6 us  [local_step(): pl.pallas_call(kernel, out_shape=(sds((N, D), BF16), sds((N, D), BF16), s...]
where the time goes in v3:
time: 36.1 us; the launch traced here: 36 us
  Pallas kernels  35.4 us (98%)
  between operations  0.64 us (2%)
    pallas_call x1, Pallas kernels, local_step(): pl.pallas_call(kernel, out_shape=(sds((N, D), BF16), sds((N, D), BF16), s...  33.6 us
    pallas_call x1, Pallas kernels, local_step(): pl.pallas_call(write_out, out_shape=(sds((N, D), BF16), sds((N, D), BF16)...  1.81 us

profile of v3, /device:TPU:0, one launch (start us, length us, event | category | flops | bytes accessed | tf_op | source)
XLA Modules:
  0.0 36.0 jit_solution(14795944608789611313)
XLA Ops:
  0.6 33.6 %xca.1 = (bf16[2048,384]{1,0:T(8,128)(2,1)S(1)}, bf16[2048,384]{1,0:T(8,128)(2,1)S(1)}, bf16[96,1152]{1,0:T(8,128)(2,1)S(1)}, bf16[96,384]{1,0:T(8,128)(2,1)S(1)...) custom-call(bf16[2048,384]{1,0:T(8,128)(2,1)} %x_hbm.1, bf16[2048,384]{1,0:T(8,128)(2,1)} %dy_hbm.1, ...), custom_call_target="tpu_custom_call" | custom-call | tf_op jit(solution)/shard_map/xca/pallas_call | solution.py:354
  34.2 1.8 %write_out.1 = (bf16[2048,384]{1,0:T(8,128)(2,1)}, bf16[2048,384]{1,0:T(8,128)(2,1)}, bf16[96,1152]{1,0:T(8,128)(2,1)}, bf16[96,384]{1,0:T(8,128)(2,1)}, f32[384]{0:T(512)}, /*index=5*/f32[384]{0:T(512)}, f32[8]{0:T(128)}) custom-call(bf16[2048,384]{1,0:T(8,128)(2,1)S(1)} %get-tuple-element.14.y, bf16[2048,384]{1,0:T(8,128)(2,1)S(1)} %get-tuple-element.15.dx, ...), custom_call_target="tpu_custom_call" | custom-call | tf_op jit(solution)/shard_map/write_out/pallas_call | solution.py:404

commit v4 on v3

--- a/solution.py
+++ b/solution.py
@@ -14,7 +14,7 @@
 GW = 192
 PW = 256
 RB = 96
-CH = 256
+CH = 512
 NCH = N // CH
 
 NN = (((1,), (0,)), ((), ()))
@@ -78,9 +78,11 @@
     s_acc[...] = jnp.zeros_like(s_acc)
     pk1[...] = jnp.zeros_like(pk1)
     pk2[...] = jnp.zeros_like(pk2)
+    es[...] = jnp.zeros_like(es)
 
     def layer_norm(i):
-        rows = pl.ds(pl.multiple_of(i * CH, CH), CH)
+        rows = pl.ds(i * CH, CH)
+        x_copy(i).wait()
         xf = x[rows, :].astype(F32)
         mean = jnp.mean(xf, axis=-1, keepdims=True)
         cen = xf - mean
@@ -90,28 +92,22 @@
         u[rows, :] = (cen * rstd * gamma[...] + beta[...]).astype(BF16)
 
     def qk_chunk(i):
-        cols = pl.ds(pl.multiple_of(i * CH, CH), CH)
+        cols = pl.ds(i * CH, CH)
         res = mm(wt[0:2 * D, :], u[cols, :], NT).astype(BF16)
         for s in range(4):
             qkvt[s // 2, s % 2, :, cols] = res[s * GW:(s + 1) * GW]
         sq = jnp.square(res.astype(F32))
-        s_acc[...] += sq[:, :128] + sq[:, 128:]
+        s_acc[...] += sum(sq[:, 128 * t:128 * t + 128] for t in range(CH // 128))
 
     gamma_copy.wait()
     beta_copy.wait()
-    x_copy(0).wait()
     layer_norm(0)
     w_copy.wait()
     wt[...] = w[...].T
-
-    @pl.loop(0, NCH - 1)
-    def _(i):
-        rows = pl.ds(pl.multiple_of((i + 1) * CH, CH), CH)
-        pltpu.make_async_copy(x_hbm.at[rows], x.at[rows], x_sem.at[i + 1]).wait()
+    for i in range(NCH):
+        if i + 1 < NCH:
+            layer_norm(i + 1)
         qk_chunk(i)
-        layer_norm(i + 1)
-
-    qk_chunk(NCH - 1)
 
     def compact(full):
         out = jnp.zeros((HD, GW), F32)
@@ -132,14 +128,9 @@
     pl.semaphore_wait(barrier, 2)
     a1 = send(0, pk1.at[peer], ra.at[0], partner)
 
-    CV = 512
-
-    @pl.loop(0, N // CV)
-    def _(i):
-        cols = pl.ds(pl.multiple_of(i * CV, CV), CV)
-        res = mm(wt[2 * D:3 * D, :], u[cols, :], NT).astype(BF16)
-        qkvt[2, 0, :, cols] = res[:GW]
-        qkvt[2, 1, :, cols] = res[GW:]
+    v_all = mm(wt[2 * D:3 * D, :], u[...], NT).astype(BF16)
+    qkvt[2, 0] = v_all[:GW]
+    qkvt[2, 1] = v_all[GW:]
 
     a1.wait_recv()
     sb[0] = pk1[core] + ra[0]
@@ -149,30 +140,21 @@
     dy_copy.wait()
     temp_copy.wait()
 
-    @pl.loop(0, N // CV)
-    def _(i):
-        cols = pl.ds(pl.multiple_of(i * CV, CV), CV)
-        res = mm(wo[...], dy[cols, :], NT).astype(BF16)
-        dot_[0, :, cols] = res[:GW]
-        dot_[1, :, cols] = res[GW:]
+    do_all = mm(wo[...], dy[...], NT).astype(BF16)
+    dot_[0] = do_all[:GW]
+    dot_[1] = do_all[GW:]
 
     for g in range(2):
         pk2[g, :, 0:GW] = compact(mm(dot_[g], qkvt[2, g], NT))
     a2 = send(2, pk2.at[peer], ra.at[1], partner)
 
-    @pl.loop(0, NCH // 2)
-    def _(i):
-        cols = pl.ds(pl.multiple_of(i * CH, CH), CH)
-        ut[:, cols] = u[cols, :].T
+    ut[:, 0:N // 2] = u[0:N // 2, :].T
 
     a2.wait_recv()
     sb[1] = pk2[core] + ra[1]
     b2 = send(3, sb.at[1], rb.at[1], other)
 
-    @pl.loop(NCH // 2, NCH)
-    def _(i):
-        cols = pl.ds(pl.multiple_of(i * CH, CH), CH)
-        ut[:, cols] = u[cols, :].T
+    ut[:, N // 2:N] = u[N // 2:N, :].T
 
     def seg_sum(v):
         out = jnp.zeros_like(v)
@@ -298,24 +280,25 @@
             dt = jnp.where(lane8 == g * 4 + h, val, dt)
     dt_out[...] = dt
 
-    es[...] = jnp.zeros_like(es)
-
-    @pl.loop(0, NCH)
-    def _(i):
-        rows = pl.ds(pl.multiple_of(i * CH, CH), CH)
-        proj = mm(ot[:, :, rows].reshape(D, CH), wo[...], TN)
-        xf = x[rows, :].astype(F32)
-        y_out[rows, :] = (xf + proj).astype(BF16)
+    ot_all = all_rows(ot)
+    x_f32 = x[...].astype(F32)
+    y_out[...] = (x_f32 + mm(ot_all, wo[...], TN)).astype(BF16)
+    dg_sum = jnp.zeros((1, D), F32)
+    db_sum = jnp.zeros((1, D), F32)
+    for i in range(NCH):
+        rows = pl.ds(i * CH, CH)
         dut = mm(w[...], dqkvt[:, :, :, rows].reshape(3 * D, CH), NN).astype(BF16)
         du = dut.T.astype(F32)
         rstd = rstd_s[rows, :]
-        xhat = (xf - mean_s[rows, :]) * rstd
-        es[0:1, :] += jnp.sum(du * xhat, axis=0, keepdims=True)
-        es[1:2, :] += jnp.sum(du, axis=0, keepdims=True)
+        xhat = (x[rows, :].astype(F32) - mean_s[rows, :]) * rstd
+        dg_sum += jnp.sum(du * xhat, axis=0, keepdims=True)
+        db_sum += jnp.sum(du, axis=0, keepdims=True)
         dh = du * gamma[...]
         m1 = jnp.mean(dh, axis=-1, keepdims=True)
         m2 = jnp.mean(dh * xhat, axis=-1, keepdims=True)
         dx_out[rows, :] = (dy[rows, :].astype(F32) + rstd * (dh - m1 - xhat * m2)).astype(BF16)
+    es[0:1, :] = dg_sum
+    es[1:2, :] = db_sum
 
     e1 = send(18, es, er.at[0], partner)
     e1.wait()

time: 36.1 us -> 32.5 us (0.900)
  Pallas kernels: 35.4 us -> 31.6 us
    pallas_call x1, Pallas kernels: 33.6 us -> 29.8 us  [local_step(): pl.pallas_call(kernel, out_shape=(sds((N, D), BF16), sds((N, D), BF16), s...]
where the time goes in v4:
time: 32.5 us; the launch traced here: 32.4 us
  Pallas kernels  31.6 us (97%)
  between operations  0.8 us (2%)
    pallas_call x1, Pallas kernels, local_step(): pl.pallas_call(kernel, out_shape=(sds((N, D), BF16), sds((N, D), BF16), s...  29.8 us
    pallas_call x1, Pallas kernels, local_step(): pl.pallas_call(write_out, out_shape=(sds((N, D), BF16), sds((N, D), BF16)...  1.81 us

profile of v4, /device:TPU:0, one launch (start us, length us, event | category | flops | bytes accessed | tf_op | source)
XLA Modules:
  0.0 32.4 jit_solution(3506648535940306730)
XLA Ops:
  0.6 29.8 %xca.1 = (bf16[2048,384]{1,0:T(8,128)(2,1)S(1)}, bf16[2048,384]{1,0:T(8,128)(2,1)S(1)}, bf16[96,1152]{1,0:T(8,128)(2,1)S(1)}, bf16[96,384]{1,0:T(8,128)(2,1)S(1)...) custom-call(bf16[2048,384]{1,0:T(8,128)(2,1)} %x_hbm.1, bf16[2048,384]{1,0:T(8,128)(2,1)} %dy_hbm.1, ...), custom_call_target="tpu_custom_call" | custom-call | tf_op jit(solution)/shard_map/xca/pallas_call | solution.py:337
  30.4 1.8 %write_out.1 = (bf16[2048,384]{1,0:T(8,128)(2,1)}, bf16[2048,384]{1,0:T(8,128)(2,1)}, bf16[96,1152]{1,0:T(8,128)(2,1)}, bf16[96,384]{1,0:T(8,128)(2,1)}, f32[384]{0:T(512)}, /*index=5*/f32[384]{0:T(512)}, f32[8]{0:T(128)}) custom-call(bf16[2048,384]{1,0:T(8,128)(2,1)S(1)} %get-tuple-element.14.y, bf16[2048,384]{1,0:T(8,128)(2,1)S(1)} %get-tuple-element.15.dx, ...), custom_call_target="tpu_custom_call" | custom-call | tf_op jit(solution)/shard_map/write_out/pallas_call | solution.py:387

commit v5 on v4

v5 whole, which is shorter than its diff:
```python
import jax
import jax.numpy as jnp
from jax import lax
from jax.experimental import pallas as pl
from jax.experimental.pallas import tpu as pltpu
from jax.sharding import PartitionSpec as P

LN_EPS = 1e-6
F32 = jnp.float32
BF16 = jnp.bfloat16
N = 2048
D = 384
HD = 48
GW = 192
PW = 256
RB = 96
CH = 512
NCH = N // CH
LEAD = 1

NN = (((1,), (0,)), ((), ()))
NT = (((1,), (1,)), ((), ()))
TN = (((0,), (0,)), ((), ()))


def mm(a, b, dims):
    return lax.dot_general(a, b, dims, preferred_element_type=F32)


def kernel(x_hbm, dy_hbm, gamma_hbm, beta_hbm, w_hbm, wo_hbm, temp_hbm,
           y_out, dx_out, dw_out, dwo_out, dg_out, db_out, dt_out,
           x, dy, w, wo, wt, u, ut, qkvt, dqkvt, dot_, ot, mean_s, rstd_s, s_acc,
           pk, ra, sb, rb, cs, rc, abd, gbd, keep, part, rd1, rd2, ls, rl, es, er,
           gamma, beta, temp, in_sem, x_sem, ssem, rsem):
    sp = lax.axis_index("sp")
    core = lax.rem(sp, 2)
    oc = 1 - lax.div(sp, 2)
    partner = sp + 1 - 2 * core
    other = lax.rem(sp + 2, 4)
    cross = lax.rem(partner + 2, 4)

    barrier = pltpu.get_barrier_semaphore()
    for dev in (partner, other):
        pl.semaphore_signal(barrier, inc=1, device_id={"sp": dev}, device_id_type=pl.DeviceIdType.MESH)

    qk_cols, v_cols = pl.ds(0, 2 * D), pl.ds(2 * D, D)
    w_copy = pltpu.make_async_copy(w_hbm.at[:, qk_cols], w.at[:, qk_cols], in_sem.at[0])
    wv_copy = pltpu.make_async_copy(w_hbm.at[:, v_cols], w.at[:, v_cols], in_sem.at[6])
    wo_copy = pltpu.make_async_copy(wo_hbm, wo, in_sem.at[1])
    dy_copy = pltpu.make_async_copy(dy_hbm, dy, in_sem.at[2])
    gamma_copy = pltpu.make_async_copy(gamma_hbm, gamma.at[0], in_sem.at[3])
    beta_copy = pltpu.make_async_copy(beta_hbm, beta.at[0], in_sem.at[4])
    temp_copy = pltpu.make_async_copy(temp_hbm, temp, in_sem.at[5])

    def x_copy(i):
        rows = pl.ds(i * CH, CH)
        return pltpu.make_async_copy(x_hbm.at[rows], x.at[rows], x_sem.at[i])

    w_copy.start()
    x_copy(0).start()
    gamma_copy.start()
    beta_copy.start()
    for i in range(1, NCH):
        x_copy(i).start()
    wv_copy.start()
    wo_copy.start()
    dy_copy.start()
    temp_copy.start()

    def remote(slot, src, dst, dev):
        return pltpu.make_async_remote_copy(
            src_ref=src, dst_ref=dst, send_sem=ssem.at[slot], recv_sem=rsem.at[slot],
            device_id={"sp": dev}, device_id_type=pl.DeviceIdType.MESH)

    def send(slot, src, dst, dev):
        copy = remote(slot, src, dst, dev)
        copy.start()
        return copy

    def on_lead(f):
        pl.when(core == LEAD)(f)

    def on_second(f):
        pl.when(core != LEAD)(f)

    a = [remote(p, pk.at[p], ra.at[p], partner) for p in range(2)]
    b = [remote(2 + p, sb.at[p], rb.at[p], other) for p in range(2)]
    c = [remote(4 + p, cs.at[p], rc.at[p], partner) for p in range(2)]

    def lead_sum(p):
        @on_lead
        def _():
            a[p].wait_recv()
            sb[p] = pk[p] + ra[p]
            b[p].start()

    lane = lax.broadcasted_iota(jnp.int32, (HD, PW), 1)
    row = lax.broadcasted_iota(jnp.int32, (HD, PW), 0)
    heads = [(lane >= HD * h) & (lane < HD * h + HD) for h in range(4)]
    eyes = [lane == row + HD * h for h in range(4)]
    valid = lane < GW
    s_acc[...] = jnp.zeros_like(s_acc)
    pk[...] = jnp.zeros_like(pk)
    es[...] = jnp.zeros_like(es)

    def layer_norm(i):
        rows = pl.ds(i * CH, CH)
        x_copy(i).wait()
        xf = x[rows, :].astype(F32)
        mean = jnp.mean(xf, axis=-1, keepdims=True)
        cen = xf - mean
        rstd = lax.rsqrt(jnp.mean(cen * cen, axis=-1, keepdims=True) + LN_EPS)
        mean_s[rows, :] = mean
        rstd_s[rows, :] = rstd
        u[rows, :] = (cen * rstd * gamma[...] + beta[...]).astype(BF16)

    def qk_chunk(i):
        cols = pl.ds(i * CH, CH)
        res = mm(wt[0:2 * D, :], u[cols, :], NT).astype(BF16)
        for s in range(4):
            qkvt[s // 2, s % 2, :, cols] = res[s * GW:(s + 1) * GW]
        sq = jnp.square(res.astype(F32))
        s_acc[...] += sum(sq[:, 128 * t:128 * t + 128] for t in range(CH // 128))

    w_copy.wait()
    wt[0:2 * D, :] = w[:, 0:2 * D].T
    gamma_copy.wait()
    beta_copy.wait()
    layer_norm(0)
    for i in range(NCH):
        if i + 1 < NCH:
            layer_norm(i + 1)
        qk_chunk(i)

    def compact(full):
        out = jnp.zeros((HD, GW), F32)
        for h in range(4):
            out = jnp.where(heads[h][:, :GW], full[HD * h:HD * h + HD], out)
        return out

    s_col = jnp.sum(s_acc[...], axis=-1, keepdims=True)
    for g in range(2):
        pk[0, g, :, 0:GW] = compact(mm(qkvt[0, g], qkvt[1, g], NT))
        blk = pk[0, g]
        for h in range(4):
            r = g * GW + h * HD
            blk = jnp.where(lane == GW + h, s_col[r:r + HD], blk)
            blk = jnp.where(lane == GW + 4 + h, s_col[D + r:D + r + HD], blk)
        pk[0, g] = blk

    pl.semaphore_wait(barrier, 2)

    @on_second
    def _():
        a[0].start()

    wv_copy.wait()
    wt[2 * D:3 * D, :] = w[:, 2 * D:3 * D].T
    v_all = mm(wt[2 * D:3 * D, :], u[...], NT).astype(BF16)
    qkvt[2, 0] = v_all[:GW]
    qkvt[2, 1] = v_all[GW:]
    lead_sum(0)

    wo_copy.wait()
    dy_copy.wait()
    temp_copy.wait()
    do_all = mm(wo[...], dy[...], NT).astype(BF16)
    dot_[0] = do_all[:GW]
    dot_[1] = do_all[GW:]
    for g in range(2):
        pk[1, g, :, 0:GW] = compact(mm(dot_[g], qkvt[2, g], NT))

    @on_second
    def _():
        a[1].start()

    u_t = u[...].T
    ut[0] = u_t[:GW]
    ut[1] = u_t[GW:]
    lead_sum(1)

    def seg_sum(v):
        out = jnp.zeros_like(v)
        for h in range(4):
            out = jnp.where(heads[h], jnp.sum(jnp.where(heads[h], v, 0.0), axis=-1, keepdims=True), out)
        return out

    def expand(dst, g, comp):
        for h in range(4):
            dst[g, HD * h:HD * h + HD, :] = jnp.where(heads[h], comp, 0.0)[:, :GW].astype(BF16)

    def softmax_fwd(g):
        gs = sb[0, g] + rb[0, g]
        rq2 = jnp.zeros((HD, PW), F32)
        rk2 = jnp.zeros((HD, PW), F32)
        tau = jnp.zeros((HD, PW), F32)
        for h in range(4):
            sq_h = jnp.sum(jnp.where(lane == GW + h, gs, 0.0), axis=-1, keepdims=True)
            sk_h = jnp.sum(jnp.where(lane == GW + 4 + h, gs, 0.0), axis=-1, keepdims=True)
            rq2 = jnp.where(heads[h], sq_h, rq2)
            rk2 = jnp.where(eyes[h], sk_h, rk2)
            tau = jnp.where(heads[h], temp[g * 4 + h], tau)
        sk2 = jnp.sum(rk2, axis=0, keepdims=True)
        q_inv = lax.rsqrt(jnp.where(valid, rq2, 1.0))
        k_inv = lax.rsqrt(jnp.where(valid, sk2, 1.0))
        gram = jnp.where(valid, gs, 0.0)
        scores = tau * gram * q_inv * k_inv
        top = jnp.zeros((HD, PW), F32)
        for h in range(4):
            top = jnp.where(heads[h], jnp.max(jnp.where(heads[h], scores, -jnp.inf), axis=-1, keepdims=True), top)
        e = jnp.where(valid, jnp.exp(scores - top), 0.0)
        prob = jnp.where(valid, e / jnp.where(valid, seg_sum(e), 1.0), 0.0)
        cs[0, g] = prob
        keep[0, g] = scores
        keep[1, g] = gram * q_inv * k_inv
        keep[2, g] = tau * q_inv * k_inv
        keep[3, g] = jnp.where(valid, rq2, 1.0)
        keep[4, g] = jnp.where(valid, jnp.broadcast_to(sk2, (HD, PW)), 1.0)

    def softmax_bwd(g):
        da = jnp.where(valid, (sb[1, g] + rb[1, g]).astype(BF16).astype(F32), 0.0)
        p = cs[0, g]
        ds = p * (da - seg_sum(da * p))
        weighted = ds * keep[0, g]
        dtemp = jnp.sum(seg_sum(ds * keep[1, g]), axis=0, keepdims=True)
        dsq = -seg_sum(weighted) / keep[3, g]
        dsk = -jnp.sum(weighted, axis=0, keepdims=True) / keep[4, g]
        blk = (ds * keep[2, g]).astype(BF16).astype(F32)
        for h in range(4):
            dsk_h = jnp.sum(jnp.where(eyes[h], dsk, 0.0), axis=-1, keepdims=True)
            dsq_h = jnp.sum(jnp.where(eyes[h], dsq, 0.0), axis=-1, keepdims=True)
            dt_h = jnp.sum(jnp.where(lane == HD * h, dtemp, 0.0), axis=-1, keepdims=True)
            blk = jnp.where(lane == GW + h, dsq_h, blk)
            blk = jnp.where(lane == GW + 4 + h, dsk_h, blk)
            blk = jnp.where(lane == GW + 8 + h, dt_h, blk)
        cs[1, g] = blk

    @on_lead
    def _():
        b[0].wait_recv()
        for g in range(2):
            softmax_fwd(g)
        c[0].start()
        for g in range(2):
            expand(abd, g, cs[0, g])

    @on_second
    def _():
        c[0].wait_recv()
        for g in range(2):
            expand(abd, g, rc[0, g])

    def attend(g):
        ot[g] = mm(abd[g], qkvt[2, g], NN).astype(BF16)

    def first_send(t):
        return send(6 + 3 * t, part.at[t, cross], rd1.at[t], partner)

    def own_send(t):
        return send(7 + 3 * t, part.at[t, partner], rd2.at[t], partner)

    def link_copy(t):
        return remote(8 + 3 * t, ls.at[t], rl.at[t], other)

    def link_send(t):
        d1[t].wait_recv()
        ls[t] = part[t, other] + rd1[t]
        link_copy(t).start()

    d1, d2 = [None] * 4, [None] * 4
    there, here = pl.ds(2 * oc, 2), pl.ds(2 - 2 * oc, 2)

    attend(oc)
    part[0, there] = mm(ot[oc], dy[...], NN).reshape(2, RB, D)
    d1[0] = first_send(0)

    @on_second
    def _():
        link_send(0)

    for g in range(2):
        dqkvt[2, g] = mm(abd[g], dot_[g], TN).astype(BF16)

    @on_lead
    def _():
        link_send(0)

    part[1, there] = mm(ut[oc], dqkvt[2].reshape(D, N), NT).reshape(2, RB, D)
    d1[1] = first_send(1)

    @on_lead
    def _():
        b[1].wait_recv()
        for g in range(2):
            softmax_bwd(g)
        c[1].start()
        rc[1] = cs[1]

    attend(1 - oc)
    part[0, here] = mm(ot[1 - oc], dy[...], NN).reshape(2, RB, D)
    d2[0] = own_send(0)
    link_send(1)

    @on_second
    def _():
        c[1].wait_recv()

    for g in range(2):
        blk = rc[1, g]
        expand(gbd, g, jnp.where(valid, blk, 0.0))
        cols = []
        for base in (GW, GW + 4):
            cols.append(jnp.concatenate(
                [jnp.sum(jnp.where(lane == base + h, blk, 0.0), axis=-1, keepdims=True) for h in range(4)], axis=0))
        dqkvt[0, g] = (mm(gbd[g], qkvt[1, g], NN) + qkvt[0, g].astype(F32) * cols[0]).astype(BF16)
        dqkvt[1, g] = (mm(gbd[g], qkvt[0, g], TN) + qkvt[1, g].astype(F32) * cols[1]).astype(BF16)

    res = mm(ut[oc], dqkvt[0:2].reshape(2 * D, N), NT)
    part[3, there] = res[:, :D].reshape(2, RB, D)
    part[2, there] = res[:, D:].reshape(2, RB, D)
    d1[2] = first_send(2)
    d1[3] = first_send(3)

    res = mm(ut[1 - oc], dqkvt[...].reshape(3 * D, N), NT)
    for t in (1, 2, 3):
        part[t, here] = res[:, D * (3 - t):D * (4 - t)].reshape(2, RB, D)
        d2[t] = own_send(t)
    link_send(2)
    link_send(3)

    lane8 = lax.broadcasted_iota(jnp.int32, (1, 8), 1)
    dt = jnp.zeros((1, 8), F32)
    for g in range(2):
        head_row = rc[1, g, 0:1, :]
        for h in range(4):
            val = jnp.sum(jnp.where(lane[0:1] == GW + 8 + h, head_row, 0.0), axis=-1, keepdims=True)
            dt = jnp.where(lane8 == g * 4 + h, val, dt)
    dt_out[...] = dt

    dg_sum = jnp.zeros((1, D), F32)
    db_sum = jnp.zeros((1, D), F32)
    for i in range(NCH):
        rows = pl.ds(i * CH, CH)
        dut = mm(w[...], dqkvt[:, :, :, rows].reshape(3 * D, CH), NN).astype(BF16)
        du = dut.T.astype(F32)
        rstd = rstd_s[rows, :]
        xhat = (x[rows, :].astype(F32) - mean_s[rows, :]) * rstd
        dg_sum += jnp.sum(du * xhat, axis=0, keepdims=True)
        db_sum += jnp.sum(du, axis=0, keepdims=True)
        dh = du * gamma[...]
        m1 = jnp.mean(dh, axis=-1, keepdims=True)
        m2 = jnp.mean(dh * xhat, axis=-1, keepdims=True)
        dx_out[rows, :] = (dy[rows, :].astype(F32) + rstd * (dh - m1 - xhat * m2)).astype(BF16)
    es[0:1, :] = dg_sum
    es[1:2, :] = db_sum
    e1 = send(18, es, er.at[0], partner)
    y_out[...] = (x[...].astype(F32) + mm(ot[...].reshape(D, N), wo[...], TN)).astype(BF16)
    e1.wait()
    er[1] = es[...] + er[0]
    e2 = send(19, er.at[1], er.at[2], other)

    outs = ((dwo_out, slice(0, D)), (dw_out, slice(2 * D, 3 * D)), (dw_out, slice(D, 2 * D)), (dw_out, slice(0, D)))
    for t in range(4):
        if t == 3:
            e2.wait()
            tot = er[1] + er[2]
            dg_out[...] = tot[0:1]
            db_out[...] = tot[1:2]
        d2[t].wait_recv()
        link_copy(t).wait_recv()
        outs[t][0][:, outs[t][1]] = (part[t, sp] + rd2[t] + rl[t]).astype(BF16)
    for t in range(4):
        for copy in (d1[t], d2[t], link_copy(t)):
            copy.wait_send()

    @on_lead
    def _():
        for p in range(2):
            b[p].wait_send()
            c[p].wait_send()

    @on_second
    def _():
        for p in range(2):
            a[p].wait_send()


def write_out(y, dx, dw, dwo, dg, db, dt, y_o, dx_o, dw_o, dwo_o, dg_o, db_o, dt_o, sem):
    copies = [pltpu.make_async_copy(src, dst, sem.at[i]) for i, (src, dst) in enumerate(
        ((y, y_o), (dx, dx_o), (dw, dw_o), (dwo, dwo_o), (dg.at[0], dg_o), (db.at[0], db_o), (dt.at[0], dt_o)))]
    for copy in copies:
        copy.start()
    for copy in copies:
        copy.wait()


def local_step(x_rows, dy_rows, ln_gamma, ln_beta, w_qkv, w_out, temperature):
    hbm = pl.BlockSpec(memory_space=pltpu.HBM)
    vmem = pl.BlockSpec(memory_space=pltpu.VMEM)
    sds = jax.ShapeDtypeStruct
    outs = pl.pallas_call(
        kernel,
        out_shape=(sds((N, D), BF16), sds((N, D), BF16), sds((RB, 3 * D), BF16), sds((RB, D), BF16),
                   sds((1, D), F32), sds((1, D), F32), sds((1, 8), F32)),
        in_specs=[hbm] * 7,
        out_specs=(vmem,) * 7,
        scratch_shapes=[
            pltpu.VMEM((N, D), BF16),
            pltpu.VMEM((N, D), BF16),
            pltpu.VMEM((D, 3 * D), BF16),
            pltpu.VMEM((D, D), BF16),
            pltpu.VMEM((3 * D, D), BF16),
            pltpu.VMEM((N, D), BF16),
            pltpu.VMEM((2, GW, N), BF16),
            pltpu.VMEM((3, 2, GW, N), BF16),
            pltpu.VMEM((3, 2, GW, N), BF16),
            pltpu.VMEM((2, GW, N), BF16),
            pltpu.VMEM((2, GW, N), BF16),
            pltpu.VMEM((N, 1), F32),
            pltpu.VMEM((N, 1), F32),
            pltpu.VMEM((2 * D, 128), F32),
            pltpu.VMEM((2, 2, HD, PW), F32),
            pltpu.VMEM((2, 2, HD, PW), F32),
            pltpu.VMEM((2, 2, HD, PW), F32),
            pltpu.VMEM((2, 2, HD, PW), F32),
            pltpu.VMEM((2, 2, HD, PW), F32),
            pltpu.VMEM((2, 2, HD, PW), F32),
            pltpu.VMEM((2, GW, GW), BF16),
            pltpu.VMEM((2, GW, GW), BF16),
            pltpu.VMEM((5, 2, HD, PW), F32),
            pltpu.VMEM((4, 4, RB, D), F32),
            pltpu.VMEM((4, RB, D), F32),
            pltpu.VMEM((4, RB, D), F32),
            pltpu.VMEM((4, RB, D), F32),
            pltpu.VMEM((4, RB, D), F32),
            pltpu.VMEM((8, D), F32),
            pltpu.VMEM((3, 8, D), F32),
            pltpu.VMEM((1, D), F32),
            pltpu.VMEM((1, D), F32),
            pltpu.SMEM((8,), F32),
            pltpu.SemaphoreType.DMA((7,)),
            pltpu.SemaphoreType.DMA((NCH,)),
            pltpu.SemaphoreType.DMA((20,)),
            pltpu.SemaphoreType.DMA((20,)),
        ],
        compiler_params=pltpu.CompilerParams(collective_id=0, has_side_effects=True, vmem_limit_bytes=48 << 20),
        name="xca",
    )(*(pltpu.with_memory_space_constraint(a, pltpu.HBM)
        for a in (x_rows, dy_rows, ln_gamma, ln_beta, w_qkv, w_out, temperature)))
    return pl.pallas_call(
        write_out,
        out_shape=(sds((N, D), BF16), sds((N, D), BF16), sds((RB, 3 * D), BF16), sds((RB, D), BF16),
                   sds((D,), F32), sds((D,), F32), sds((8,), F32)),
        in_specs=[pl.BlockSpec(memory_space=pl.ANY)] * 7,
        out_specs=(hbm,) * 7,
        scratch_shapes=[pltpu.SemaphoreType.DMA((7,))],
        compiler_params=pltpu.CompilerParams(vmem_limit_bytes=1 << 20),
        name="write_out",
    )(*outs)


def solution(mesh):
    row_spec = P(('dp', 'sp'), None)
    full_mat = P(None, None)
    full_vec = P(None)
    part_vec = P('dp')
    return jax.shard_map(local_step, mesh=mesh,
                         in_specs=(row_spec, row_spec, full_vec, full_vec, full_mat, full_mat, full_vec),
                         out_specs=(row_spec, row_spec, row_spec, row_spec, part_vec, part_vec, part_vec),
                         check_vma=False)
```

time: 32.5 us -> 32.4 us (level)
  no operation moved by 1% of the time
where the time goes in v5:
time: 32.4 us; the launch traced here: 32.2 us
  Pallas kernels  31.4 us (97%)
  between operations  0.8 us (2%)
    pallas_call x1, Pallas kernels, local_step(): pl.pallas_call(kernel, out_shape=(sds((N, D), BF16), sds((N, D), BF16), s...  29.6 us
    pallas_call x1, Pallas kernels, local_step(): pl.pallas_call(write_out, out_shape=(sds((N, D), BF16), sds((N, D), BF16)...  1.81 us

profile of v5, /device:TPU:0, one launch (start us, length us, event | category | flops | bytes accessed | tf_op | source)
XLA Modules:
  0.0 32.2 jit_solution(17925777308385686811)
XLA Ops:
  0.6 29.6 %xca.1 = (bf16[2048,384]{1,0:T(8,128)(2,1)S(1)}, bf16[2048,384]{1,0:T(8,128)(2,1)S(1)}, bf16[96,1152]{1,0:T(8,128)(2,1)S(1)}, bf16[96,384]{1,0:T(8,128)(2,1)S(1)...) custom-call(bf16[2048,384]{1,0:T(8,128)(2,1)} %x_hbm.1, bf16[2048,384]{1,0:T(8,128)(2,1)} %dy_hbm.1, ...), custom_call_target="tpu_custom_call" | custom-call | tf_op jit(solution)/shard_map/xca/pallas_call | solution.py:401
  30.3 1.8 %write_out.1 = (bf16[2048,384]{1,0:T(8,128)(2,1)}, bf16[2048,384]{1,0:T(8,128)(2,1)}, bf16[96,1152]{1,0:T(8,128)(2,1)}, bf16[96,384]{1,0:T(8,128)(2,1)}, f32[384]{0:T(512)}, /*index=5*/f32[384]{0:T(512)}, f32[8]{0:T(128)}) custom-call(bf16[2048,384]{1,0:T(8,128)(2,1)S(1)} %get-tuple-element.14.y, bf16[2048,384]{1,0:T(8,128)(2,1)S(1)} %get-tuple-element.15.dx, ...), custom_call_target="tpu_custom_call" | custom-call | tf_op jit(solution)/shard_map/write_out/pallas_call | solution.py:450

commit v6 on v5

--- a/solution.py
+++ b/solution.py
@@ -16,7 +16,7 @@
 RB = 96
 CH = 512
 NCH = N // CH
-LEAD = 1
+LEAD = 0
 
 NN = (((1,), (0,)), ((), ()))
 NT = (((1,), (1,)), ((), ()))
@@ -40,7 +40,7 @@
     cross = lax.rem(partner + 2, 4)
 
     barrier = pltpu.get_barrier_semaphore()
-    for dev in (partner, other):
+    for dev in (partner, other, cross):
         pl.semaphore_signal(barrier, inc=1, device_id={"sp": dev}, device_id_type=pl.DeviceIdType.MESH)
 
     qk_cols, v_cols = pl.ds(0, 2 * D), pl.ds(2 * D, D)
@@ -101,7 +101,6 @@
     valid = lane < GW
     s_acc[...] = jnp.zeros_like(s_acc)
     pk[...] = jnp.zeros_like(pk)
-    es[...] = jnp.zeros_like(es)
 
     def layer_norm(i):
         rows = pl.ds(i * CH, CH)
@@ -148,7 +147,7 @@
             blk = jnp.where(lane == GW + 4 + h, s_col[D + r:D + r + HD], blk)
         pk[0, g] = blk
 
-    pl.semaphore_wait(barrier, 2)
+    pl.semaphore_wait(barrier, 3)
 
     @on_second
     def _():
@@ -156,10 +155,13 @@
 
     wv_copy.wait()
     wt[2 * D:3 * D, :] = w[:, 2 * D:3 * D].T
+    u_t = u[...].T
+    ut[0] = u_t[:GW]
+    ut[1] = u_t[GW:]
+    lead_sum(0)
     v_all = mm(wt[2 * D:3 * D, :], u[...], NT).astype(BF16)
     qkvt[2, 0] = v_all[:GW]
     qkvt[2, 1] = v_all[GW:]
-    lead_sum(0)
 
     wo_copy.wait()
     dy_copy.wait()
@@ -174,9 +176,6 @@
     def _():
         a[1].start()
 
-    u_t = u[...].T
-    ut[0] = u_t[:GW]
-    ut[1] = u_t[GW:]
     lead_sum(1)
 
     def seg_sum(v):
@@ -281,12 +280,12 @@
     for g in range(2):
         dqkvt[2, g] = mm(abd[g], dot_[g], TN).astype(BF16)
 
-    @on_lead
-    def _():
-        link_send(0)
-
     part[1, there] = mm(ut[oc], dqkvt[2].reshape(D, N), NT).reshape(2, RB, D)
     d1[1] = first_send(1)
+
+    @on_second
+    def _():
+        link_send(1)
 
     @on_lead
     def _():
@@ -299,7 +298,10 @@
     attend(1 - oc)
     part[0, here] = mm(ot[1 - oc], dy[...], NN).reshape(2, RB, D)
     d2[0] = own_send(0)
-    link_send(1)
+
+    @on_lead
+    def _():
+        link_send(0)
 
     @on_second
     def _():
@@ -315,19 +317,16 @@
         dqkvt[0, g] = (mm(gbd[g], qkvt[1, g], NN) + qkvt[0, g].astype(F32) * cols[0]).astype(BF16)
         dqkvt[1, g] = (mm(gbd[g], qkvt[0, g], TN) + qkvt[1, g].astype(F32) * cols[1]).astype(BF16)
 
+    @on_lead
+    def _():
+        link_send(1)
+
     res = mm(ut[oc], dqkvt[0:2].reshape(2 * D, N), NT)
     part[3, there] = res[:, :D].reshape(2, RB, D)
     part[2, there] = res[:, D:].reshape(2, RB, D)
     d1[2] = first_send(2)
     d1[3] = first_send(3)
 
-    res = mm(ut[1 - oc], dqkvt[...].reshape(3 * D, N), NT)
-    for t in (1, 2, 3):
-        part[t, here] = res[:, D * (3 - t):D * (4 - t)].reshape(2, RB, D)
-        d2[t] = own_send(t)
-    link_send(2)
-    link_send(3)
-
     lane8 = lax.broadcasted_iota(jnp.int32, (1, 8), 1)
     dt = jnp.zeros((1, 8), F32)
     for g in range(2):
@@ -340,6 +339,12 @@
     dg_sum = jnp.zeros((1, D), F32)
     db_sum = jnp.zeros((1, D), F32)
     for i in range(NCH):
+        if i == NCH // 2:
+            @on_lead
+            def _():
+                link_send(2)
+                link_send(3)
+
         rows = pl.ds(i * CH, CH)
         dut = mm(w[...], dqkvt[:, :, :, rows].reshape(3 * D, CH), NN).astype(BF16)
         du = dut.T.astype(F32)
@@ -353,20 +358,28 @@
         dx_out[rows, :] = (dy[rows, :].astype(F32) + rstd * (dh - m1 - xhat * m2)).astype(BF16)
     es[0:1, :] = dg_sum
     es[1:2, :] = db_sum
-    e1 = send(18, es, er.at[0], partner)
+    ecopies = [send(18 + i, es, er.at[i], dev) for i, dev in enumerate((partner, other, cross))]
+
+    @on_second
+    def _():
+        link_send(2)
+        link_send(3)
+
+    res = mm(ut[1 - oc], dqkvt[...].reshape(3 * D, N), NT)
+    for t in (1, 2, 3):
+        part[t, here] = res[:, D * (3 - t):D * (4 - t)].reshape(2, RB, D)
+        d2[t] = own_send(t)
     y_out[...] = (x[...].astype(F32) + mm(ot[...].reshape(D, N), wo[...], TN)).astype(BF16)
-    e1.wait()
-    er[1] = es[...] + er[0]
-    e2 = send(19, er.at[1], er.at[2], other)
 
     outs = ((dwo_out, slice(0, D)), (dw_out, slice(2 * D, 3 * D)), (dw_out, slice(D, 2 * D)), (dw_out, slice(0, D)))
     for t in range(4):
-        if t == 3:
-            e2.wait()
-            tot = er[1] + er[2]
-            dg_out[...] = tot[0:1]
-            db_out[...] = tot[1:2]
         d2[t].wait_recv()
+    for copy in ecopies:
+        copy.wait()
+    tot = (es[...] + er[0]) + (er[1] + er[2])
+    dg_out[...] = tot[0:1]
+    db_out[...] = tot[1:2]
+    for t in range(4):
         link_copy(t).wait_recv()
         outs[t][0][:, outs[t][1]] = (part[t, sp] + rd2[t] + rl[t]).astype(BF16)
     for t in range(4):
@@ -433,15 +446,15 @@
             pltpu.VMEM((4, RB, D), F32),
             pltpu.VMEM((4, RB, D), F32),
             pltpu.VMEM((4, RB, D), F32),
-            pltpu.VMEM((8, D), F32),
-            pltpu.VMEM((3, 8, D), F32),
+            pltpu.VMEM((2, D), F32),
+            pltpu.VMEM((3, 2, D), F32),
             pltpu.VMEM((1, D), F32),
             pltpu.VMEM((1, D), F32),
             pltpu.SMEM((8,), F32),
             pltpu.SemaphoreType.DMA((7,)),
             pltpu.SemaphoreType.DMA((NCH,)),
-            pltpu.SemaphoreType.DMA((20,)),
-            pltpu.SemaphoreType.DMA((20,)),
+            pltpu.SemaphoreType.DMA((21,)),
+            pltpu.SemaphoreType.DMA((21,)),
         ],
         compiler_params=pltpu.CompilerParams(collective_id=0, has_side_effects=True, vmem_limit_bytes=48 << 20),
         name="xca",

time: 32.4 us -> 30.5 us (0.941)
  the two profiles are of different devices: /device:TPU:0 before, /device:TPU:1 now
where the time goes in v6:
time: 30.5 us; the launch traced here: 30.3 us
  Pallas kernels  29.5 us (97%)
  between operations  0.8 us (3%)
    pallas_call x1, Pallas kernels, local_step(): pl.pallas_call(kernel, out_shape=(sds((N, D), BF16), sds((N, D), BF16), s...  27.7 us
    pallas_call x1, Pallas kernels, local_step(): pl.pallas_call(write_out, out_shape=(sds((N, D), BF16), sds((N, D), BF16)...  1.81 us

profile of v6, /device:TPU:1, one launch (start us, length us, event | category | flops | bytes accessed | tf_op | source)
XLA Modules:
  0.0 30.3 jit_solution(12312291920212703129)
XLA Ops:
  0.6 27.7 %xca.1 = (bf16[2048,384]{1,0:T(8,128)(2,1)S(1)}, bf16[2048,384]{1,0:T(8,128)(2,1)S(1)}, bf16[96,1152]{1,0:T(8,128)(2,1)S(1)}, bf16[96,384]{1,0:T(8,128)(2,1)S(1)...) custom-call(bf16[2048,384]{1,0:T(8,128)(2,1)} %x_hbm.1, bf16[2048,384]{1,0:T(8,128)(2,1)} %dy_hbm.1, ...), custom_call_target="tpu_custom_call" | custom-call | tf_op jit(solution)/shard_map/xca/pallas_call | solution.py:414
  28.4 1.8 %write_out.1 = (bf16[2048,384]{1,0:T(8,128)(2,1)}, bf16[2048,384]{1,0:T(8,128)(2,1)}, bf16[96,1152]{1,0:T(8,128)(2,1)}, bf16[96,384]{1,0:T(8,128)(2,1)}, f32[384]{0:T(512)}, /*index=5*/f32[384]{0:T(512)}, f32[8]{0:T(128)}) custom-call(bf16[2048,384]{1,0:T(8,128)(2,1)S(1)} %get-tuple-element.14.y, bf16[2048,384]{1,0:T(8,128)(2,1)S(1)} %get-tuple-element.15.dx, ...), custom_call_target="tpu_custom_call" | custom-call | tf_op jit(solution)/shard_map/write_out/pallas_call | solution.py:463

commit v7 on v6

--- a/solution.py
+++ b/solution.py
@@ -16,6 +16,8 @@
 RB = 96
 CH = 512
 NCH = N // CH
+STARTS = (0, 512, 1024)
+SIZES = (512, 512, 1024)
 LEAD = 0
 
 NN = (((1,), (0,)), ((), ()))
@@ -53,14 +55,14 @@
     temp_copy = pltpu.make_async_copy(temp_hbm, temp, in_sem.at[5])
 
     def x_copy(i):
-        rows = pl.ds(i * CH, CH)
+        rows = pl.ds(STARTS[i], SIZES[i])
         return pltpu.make_async_copy(x_hbm.at[rows], x.at[rows], x_sem.at[i])
 
     w_copy.start()
     x_copy(0).start()
     gamma_copy.start()
     beta_copy.start()
-    for i in range(1, NCH):
+    for i in range(1, len(SIZES)):
         x_copy(i).start()
     wv_copy.start()
     wo_copy.start()
@@ -103,7 +105,7 @@
     pk[...] = jnp.zeros_like(pk)
 
     def layer_norm(i):
-        rows = pl.ds(i * CH, CH)
+        rows = pl.ds(STARTS[i], SIZES[i])
         x_copy(i).wait()
         xf = x[rows, :].astype(F32)
         mean = jnp.mean(xf, axis=-1, keepdims=True)
@@ -114,20 +116,20 @@
         u[rows, :] = (cen * rstd * gamma[...] + beta[...]).astype(BF16)
 
     def qk_chunk(i):
-        cols = pl.ds(i * CH, CH)
+        cols = pl.ds(STARTS[i], SIZES[i])
         res = mm(wt[0:2 * D, :], u[cols, :], NT).astype(BF16)
         for s in range(4):
             qkvt[s // 2, s % 2, :, cols] = res[s * GW:(s + 1) * GW]
         sq = jnp.square(res.astype(F32))
-        s_acc[...] += sum(sq[:, 128 * t:128 * t + 128] for t in range(CH // 128))
+        s_acc[...] += sum(sq[:, 128 * t:128 * t + 128] for t in range(SIZES[i] // 128))
 
     w_copy.wait()
     wt[0:2 * D, :] = w[:, 0:2 * D].T
     gamma_copy.wait()
     beta_copy.wait()
     layer_norm(0)
-    for i in range(NCH):
-        if i + 1 < NCH:
+    for i in range(len(SIZES)):
+        if i + 1 < len(SIZES):
             layer_norm(i + 1)
         qk_chunk(i)
 
@@ -280,8 +282,9 @@
     for g in range(2):
         dqkvt[2, g] = mm(abd[g], dot_[g], TN).astype(BF16)
 
-    part[1, there] = mm(ut[oc], dqkvt[2].reshape(D, N), NT).reshape(2, RB, D)
+    part[1] = mm(ut[...].reshape(D, N), dqkvt[2].reshape(D, N), NT).reshape(4, RB, D)
     d1[1] = first_send(1)
+    d2[1] = own_send(1)
 
     @on_second
     def _():
@@ -294,14 +297,6 @@
             softmax_bwd(g)
         c[1].start()
         rc[1] = cs[1]
-
-    attend(1 - oc)
-    part[0, here] = mm(ot[1 - oc], dy[...], NN).reshape(2, RB, D)
-    d2[0] = own_send(0)
-
-    @on_lead
-    def _():
-        link_send(0)
 
     @on_second
     def _():
@@ -319,13 +314,18 @@
 
     @on_lead
     def _():
-        link_send(1)
+        link_send(0)
 
     res = mm(ut[oc], dqkvt[0:2].reshape(2 * D, N), NT)
     part[3, there] = res[:, :D].reshape(2, RB, D)
     part[2, there] = res[:, D:].reshape(2, RB, D)
     d1[2] = first_send(2)
     d1[3] = first_send(3)
+
+    @on_lead
+    def _():
+        link_send(1)
+
 
     lane8 = lax.broadcasted_iota(jnp.int32, (1, 8), 1)
     dt = jnp.zeros((1, 8), F32)
@@ -365,8 +365,11 @@
         link_send(2)
         link_send(3)
 
-    res = mm(ut[1 - oc], dqkvt[...].reshape(3 * D, N), NT)
-    for t in (1, 2, 3):
+    attend(1 - oc)
+    part[0, here] = mm(ot[1 - oc], dy[...], NN).reshape(2, RB, D)
+    d2[0] = own_send(0)
+    res = mm(ut[1 - oc], dqkvt[0:2].reshape(2 * D, N), NT)
+    for t in (2, 3):
         part[t, here] = res[:, D * (3 - t):D * (4 - t)].reshape(2, RB, D)
         d2[t] = own_send(t)
     y_out[...] = (x[...].astype(F32) + mm(ot[...].reshape(D, N), wo[...], TN)).astype(BF16)

time: 30.5 us -> 29.9 us (0.980)
  Pallas kernels: 29.5 us -> 28.9 us
    pallas_call x1, Pallas kernels: 27.7 us -> 27.1 us  [local_step(): pl.pallas_call(kernel, out_shape=(sds((N, D), BF16), sds((N, D), BF16), s...]
where the time goes in v7:
time: 29.9 us; the launch traced here: 29.8 us
  Pallas kernels  28.9 us (97%)
  between operations  0.8 us (3%)
    pallas_call x1, Pallas kernels, local_step(): pl.pallas_call(kernel, out_shape=(sds((N, D), BF16), sds((N, D), BF16), s...  27.1 us
    pallas_call x1, Pallas kernels, local_step(): pl.pallas_call(write_out, out_shape=(sds((N, D), BF16), sds((N, D), BF16)...  1.81 us

profile of v7, /device:TPU:1, one launch (start us, length us, event | category | flops | bytes accessed | tf_op | source)
XLA Modules:
  0.0 29.8 jit_solution(3810872858551792140)
XLA Ops:
  0.6 27.1 %xca.1 = (bf16[2048,384]{1,0:T(8,128)(2,1)S(1)}, bf16[2048,384]{1,0:T(8,128)(2,1)S(1)}, bf16[96,1152]{1,0:T(8,128)(2,1)S(1)}, bf16[96,384]{1,0:T(8,128)(2,1)S(1)...) custom-call(bf16[2048,384]{1,0:T(8,128)(2,1)} %x_hbm.1, bf16[2048,384]{1,0:T(8,128)(2,1)} %dy_hbm.1, ...), custom_call_target="tpu_custom_call" | custom-call | tf_op jit(solution)/shard_map/xca/pallas_call | solution.py:417
  27.8 1.8 %write_out.1 = (bf16[2048,384]{1,0:T(8,128)(2,1)}, bf16[2048,384]{1,0:T(8,128)(2,1)}, bf16[96,1152]{1,0:T(8,128)(2,1)}, bf16[96,384]{1,0:T(8,128)(2,1)}, f32[384]{0:T(512)}, /*index=5*/f32[384]{0:T(512)}, f32[8]{0:T(128)}) custom-call(bf16[2048,384]{1,0:T(8,128)(2,1)S(1)} %get-tuple-element.14.y, bf16[2048,384]{1,0:T(8,128)(2,1)S(1)} %get-tuple-element.15.dx, ...), custom_call_target="tpu_custom_call" | custom-call | tf_op jit(solution)/shard_map/write_out/pallas_call | solution.py:466
